TPU v7x, 8 devices: a whole 2x2x1 slice. The times are simulated.
8 devices in a mesh: cz: 2 (over z, y), cy: 2 (over x), cx: 2 (over core).
Axes of the slice: x: 2, y: 2, z: 1, core: 2. Of those that a mesh axis runs over, the one named last changes fastest.
Arguments:
- x: bfloat16 [768, 3072], P(('cx', 'cz'), 'cy')
- w1: bfloat16 [3072, 12288], P('cy', ('cz', 'cx'))
- w2: bfloat16 [12288, 3072], P('cz', ('cy', 'cx'))
Outputs:
- output: bfloat16 [768, 3072], P(('cx', 'cz'), 'cy')
All inputs are finite; a program needn't handle non-finite values.
Results may differ from a plain program's by a relative error of at most 0.0115081.
Values are sent between devices in bfloat16 or wider.
A program may use at most 1 GiB of HBM per device.

v0:
```python
import jax
import jax.numpy as jnp
from jax import lax
from jax.sharding import PartitionSpec as P


def solution(mesh):
    def body(x, w1, w2):
        xg = lax.all_gather(x, "cz", axis=0, tiled=True)
        w1g = lax.all_gather(w1, "cx", axis=1, tiled=True)
        cp = jnp.dot(xg, w1g, preferred_element_type=jnp.float32)
        c = lax.psum_scatter(cp, "cy", scatter_dimension=0, tiled=True).astype(jnp.bfloat16)
        h = jax.nn.gelu(c.astype(jnp.float32), approximate=True).astype(jnp.bfloat16)
        hg = lax.all_gather(h, "cy", axis=0, tiled=True)
        w2g = lax.all_gather(w2, "cx", axis=1, tiled=True)
        zp = jnp.dot(hg, w2g, preferred_element_type=jnp.float32)
        return lax.psum_scatter(zp, "cz", scatter_dimension=0, tiled=True).astype(jnp.bfloat16)

    return jax.shard_map(
        body,
        mesh=mesh,
        in_specs=(P(("cx", "cz"), "cy"), P("cy", ("cz", "cx")), P("cz", ("cy", "cx"))),
        out_specs=P(("cx", "cz"), "cy"),
        check_vma=False,
    )
```

profile of v0, /device:TPU:0, one launch (start us, length us, event | category | flops | bytes accessed | tf_op | source)
XLA Modules:
  0.0 337.6 jit_solution(8626687349470149724)
XLA Ops:
  6.5 0.0 all-gather.5.cloned.1.call-start
  6.5 0.7 all-gather.5.cloned.1.call-update
  7.3 0.0 all-gather.7.cloned.1.call-start
  7.3 0.7 all-gather.7.cloned.1.call-update
  8.0 0.0 reduce-scatter.3.cloned.1.call-start
  8.1 23.3 %all-gather.5.cloned.1.call-done = bf16[384,1536]{1,0:T(8,128)(2,1)} async-done(((bf16[192,1536]{1,0:T(8,128)(2,1)}), bf16[384,1536]{1,0:T(8,128)(2,1)}) %all-gather.5.cloned.1.call-update) | async-done | bytes 1179664 | tf_op jit(solution)/shard_map/all_gather | solution.py:9
  31.3 32.9 %all-gather.7.cloned.1.call-done = bf16[1536,6144]{1,0:T(8,128)(2,1)} async-done(((bf16[1536,3072]{1,0:T(8,128)(2,1)}), bf16[1536,6144]{1,0:T(8,128)(2,1)}) %all-gather.7.cloned.1.call-update) | async-done | bytes 18874384 | tf_op jit(solution)/shard_map/all_gather | solution.py:10
  64.2 13.8 %fusion.6 = f32[384,6144]{1,0:T(8,128)} fusion(bf16[384,1536]{1,0:T(8,128)(2,1)} %all-gather.5.cloned.1.call-done, bf16[1536,6144]{1,0:T(8,128)(2,1)} %all-gather.7.cloned.1.call-done), kind=kOutput, calls=%fused_computation.10 | convolution fusion | flops 7247757312 | bytes 29491200 | tf_op jit(solution)/shard_map/dot_general | solution.py:11
  78.0 0.0 reduce-scatter.3.cloned.1.call-update
  78.1 0.0 all-gather.11.cloned.1.call-start
  78.1 0.5 all-gather.11.cloned.1.call-update
  78.6 0.0 all-gather.9.cloned.1.call-start
  78.7 108.5 %reduce-scatter.3.cloned.1.call-done = f32[192,6144]{1,0:T(8,128)} async-done(((f32[384,6144]{1,0:T(8,128)}), f32[192,6144]{1,0:T(8,128)}) %reduce-scatter.3.cloned.1.call-update) | async-done | bytes 4718608 | tf_op jit(solution)/shard_map/reduce_scatter | solution.py:12
  187.1 5.2 %fusion.5 = bf16[192,6144]{1,0:T(8,128)(2,1)} fusion(f32[192,6144]{1,0:T(8,128)} %reduce-scatter.3.cloned.1.call-done), kind=kLoop, calls=%fused_computation.9 | loop fusion | flops 12976128 | bytes 7077888 | tf_op jit(solution)/shard_map/convert_element_type | solution.py:13
  192.4 0.0 all-gather.9.cloned.1.call-update
  192.4 0.0 reduce-scatter.5.cloned.1.call-start
  192.4 27.5 %all-gather.11.cloned.1.call-done = bf16[6144,1536]{1,0:T(8,128)(2,1)} async-done(((bf16[6144,768]{1,0:T(8,128)(2,1)}), bf16[6144,1536]{1,0:T(8,128)(2,1)}) %all-gather.11.cloned.1.call-update) | async-done | bytes 18874384 | tf_op jit(solution)/shard_map/all_gather | solution.py:15
  219.9 62.7 %all-gather.9.cloned.1.call-done = bf16[384,6144]{1,0:T(8,128)(2,1)} async-done(((bf16[192,6144]{1,0:T(8,128)(2,1)}), bf16[384,6144]{1,0:T(8,128)(2,1)}) %all-gather.9.cloned.1.call-update) | async-done | bytes 4718608 | tf_op jit(solution)/shard_map/all_gather | solution.py:14
  282.6 13.9 %fusion.7 = f32[384,1536]{1,0:T(8,128)} fusion(bf16[384,6144]{1,0:T(8,128)(2,1)} %all-gather.9.cloned.1.call-done, bf16[6144,1536]{1,0:T(8,128)(2,1)} %all-gather.11.cloned.1.call-done), kind=kOutput, calls=%fused_computation.11 | convolution fusion | flops 7247757312 | bytes 25952256 | tf_op jit(solution)/shard_map/dot_general | solution.py:16
  296.5 0.0 reduce-scatter.5.cloned.1.call-update
  296.5 32.1 %reduce-scatter.5.cloned.1.call-done = f32[192,1536]{1,0:T(8,128)} async-done(((f32[384,1536]{1,0:T(8,128)}), f32[192,1536]{1,0:T(8,128)}) %reduce-scatter.5.cloned.1.call-update) | async-done | bytes 1179664 | tf_op jit(solution)/shard_map/reduce_scatter | solution.py:17
  328.6 2.1 convert_element_type.15
Async XLA Ops:
  6.5 24.8 %all-gather.5.cloned.1.call-start = ((), (), s32[]{:S(2)}) async-start(), calls=%async_computation.2 | async-start | bytes 1769472 | tf_op jit(solution)/shard_map/all_gather | solution.py:9
  7.3 56.9 %all-gather.7.cloned.1.call-start = ((), (), s32[]{:S(2)}) async-start(), calls=%async_computation.3 | async-start | bytes 28311552 | tf_op jit(solution)/shard_map/all_gather | solution.py:10
  8.0 179.1 %reduce-scatter.3.cloned.1.call-start = ((), (), s32[]{:S(2)}) async-start(), calls=%async_computation.4 | async-start | bytes 14155776 | tf_op jit(solution)/shard_map/reduce_scatter | solution.py:12
  78.1 141.8 %all-gather.11.cloned.1.call-start = ((), (), s32[]{:S(2)}) async-start(), calls=%async_computation.6 | async-start | bytes 28311552 | tf_op jit(solution)/shard_map/all_gather | solution.py:15
  78.6 204.0 %all-gather.9.cloned.1.call-start = ((), (), s32[]{:S(2)}) async-start(), calls=%async_computation.5 | async-start | bytes 7077888 | tf_op jit(solution)/shard_map/all_gather | solution.py:14
  192.4 136.2 %reduce-scatter.5.cloned.1.call-start = ((), (), s32[]{:S(2)}) async-start(), calls=%async_computation.7 | async-start | bytes 3538944 | tf_op jit(solution)/shard_map/reduce_scatter | solution.py:17
Sparse Core Ops, SparseCore 0:
  8.8 22.4 all-gather.4
  32.8 31.3 all-gather.6
  78.2 108.9 reduce-scatter.2
  188.5 31.3 all-gather.10
  221.2 61.3 all-gather.8
  296.7 31.9 reduce-scatter.4
where the time goes:
time: 338 us
  waiting for transfers between devices  289 us (86%)
  matrix products  27.7 us (8%)
  between operations  13.5 us (4%)
  other arithmetic  7.37 us (2%)
    reduce_scatter x1, waiting for transfers between devices, body(): lax.psum_scatter(cp, 'cy', scatter_dimension=0, tiled=True)  108 us
    all_gather x1, waiting for transfers between devices, body(): hg = lax.all_gather(h, 'cy', axis=0, tiled=True)  62.7 us
    all_gather x1, waiting for transfers between devices, body(): w1g = lax.all_gather(w1, 'cx', axis=1, tiled=True)  32.9 us
    reduce_scatter x1, waiting for transfers between devices, body(): lax.psum_scatter(zp, 'cz', scatter_dimension=0, tiled=True)  32.1 us
    all_gather x1, waiting for transfers between devices, body(): w2g = lax.all_gather(w2, 'cx', axis=1, tiled=True)  27.5 us
    all_gather x1, waiting for transfers between devices, body(): xg = lax.all_gather(x, 'cz', axis=0, tiled=True)  23.3 us
    dot_general x1, matrix products, body(): zp = jnp.dot(hg, w2g, preferred_element_type=jnp.float32)  13.9 us
    dot_general x1, matrix products, body(): cp = jnp.dot(xg, w1g, preferred_element_type=jnp.float32)  13.8 us
  transfers between devices with their start and end apart: 6, of which 6 were waited for; matrix products, arithmetic and copies ran while one was open for 2% of the time, Pallas kernels for 0%

commit v1 on v0

v1 whole, which is shorter than its diff:
```python
import math

import jax
import jax.numpy as jnp
from jax import lax
from jax.experimental import pallas as pl
from jax.experimental.pallas import tpu as pltpu
from jax.sharding import PartitionSpec as P

MESH = pl.DeviceIdType.MESH
F32 = jnp.float32
BF16 = jnp.bfloat16
M = 64
TILE = 512


def gelu_tanh(c):
    return 0.5 * c * (1.0 + jnp.tanh(math.sqrt(2 / math.pi) * (c + 0.044715 * (c * c * c))))


def kernel(x, w1, w2, z, xv, w1v, w2v, ps, pr, po, ho, hr, zs, zr, ov,
           xl_sem, w1_sem, w2_sem, out_sem, bx_send, bx_recv, bw_send, bw_recv,
           xy_send, xy_recv, xf_send, xf_recv, p_send, p_recv, h_send, h_recv, z_send, z_recv):
    cz, cy, cx = lax.axis_index("cz"), lax.axis_index("cy"), lax.axis_index("cx")
    across = {"cy": 1 - cy}
    partner = {"cx": 1 - cx}
    along = {"cz": 1 - cz}
    diagonal = {"cz": 1 - cz, "cx": 1 - cx}
    rows, half = x.shape
    chunks = 4 * rows // M
    per = rows // M

    def remote(src, dst, send, recv, device):
        return pltpu.make_async_remote_copy(src_ref=src, dst_ref=dst, send_sem=send, recv_sem=recv,
                                            device_id=device, device_id_type=MESH)

    def at(i, n=M):
        return pl.ds(pl.multiple_of(i * M, M), n)

    x_first = pltpu.make_async_copy(x.at[pl.ds(0, M)], xv.at[pl.ds(0, M)], xl_sem.at[0])
    x_last = pltpu.make_async_copy(x.at[pl.ds(M, rows - M)], xv.at[pl.ds(10 * M, rows - M)], xl_sem.at[1])
    cols = lambda side: pl.ds(pl.multiple_of(side * half, half), half)
    w1_send = pltpu.make_async_copy(w1.at[:, cols(1 - cy)], w1v.at[0], w1_sem.at[0])
    w1_keep = pltpu.make_async_copy(w1.at[:, cols(cy)], w1v.at[1], w1_sem.at[1])
    width = w2.shape[1]

    def w2_rows(core, k):
        side = cy if k == 0 else 1 - cy
        return w2.at[pl.ds(pl.multiple_of((core * 2 + side) * half, half), half)]

    mine = pl.ds(pl.multiple_of(cx * width, width), width)
    w2_local = [pltpu.make_async_copy(w2_rows(cx, k), w2v.at[k, :, mine], w2_sem.at[k]) for k in range(2)]
    w2_swap = [remote(w2_rows(1 - cx, k), w2v.at[k, :, mine], bw_send.at[k], bw_recv.at[k], partner) for k in range(2)]
    x_swap = [
        remote(x.at[pl.ds(0, M)], xv.at[pl.ds(M, M)], bx_send.at[0], bx_recv.at[0], partner),
        remote(x.at[pl.ds(M, rows - M)], xv.at[pl.ds(8 * M, rows - M)], bx_send.at[1], bx_recv.at[1], partner),
    ]
    x_along = [remote(x.at[pl.ds(k * M, M)], xv.at[pl.ds((2 + k) * M, M)], xy_send.at[k], xy_recv.at[k], along)
               for k in range(per)]

    def x_forward(k):
        return remote(xv.at[at(2 + k)], xv.at[at(5 + k)], xf_send.at[k], xf_recv.at[k], partner)

    def p_copy(i):
        return remote(ps.at[at(i)], pr.at[at(i)], p_send.at[i], p_recv.at[i], across)

    def h_copy(i):
        return remote(ho.at[at(i)], hr.at[at(i)], h_send.at[i], h_recv.at[i], across)

    def z_copy(i, slot, row, device):
        return remote(zs.at[at(i)], zr.at[slot, at(row)], z_send.at[i], z_recv.at[i], device)

    x_first.start()
    w1_send.start()
    x_last.start()
    w1_keep.start()

    barrier = pltpu.get_barrier_semaphore()
    for device in (across, partner, along, diagonal):
        pl.semaphore_signal(barrier, inc=1, device_id=device, device_id_type=MESH)
    pl.semaphore_wait(barrier, 4)

    for copy in x_along:
        copy.start()
    for copy in x_swap:
        copy.start()

    def first_layer(i, side, out, out_rows):
        for n in range(half // TILE):
            c = pl.ds(n * TILE, TILE)
            out[out_rows, c] = jnp.dot(xv[at(i), :], w1v[side, :, c], preferred_element_type=F32)

    def partial(i):
        @pl.when(i == 0)
        def _():
            x_first.wait()
            w1_send.wait()

        @pl.when(i == 1)
        def _():
            x_swap[0].wait_recv()

        @pl.when((i >= 2) & (i < 5))
        def _():
            k = i - 2
            remote(xv.at[at(i)], xv.at[at(i)], xy_send.at[k], xy_recv.at[k], along).wait_recv()
            x_forward(k).start()

        @pl.when((i >= 5) & (i < 8))
        def _():
            x_forward(i - 5).wait_recv()

        @pl.when(i == 8)
        def _():
            x_swap[1].wait_recv()

        @pl.when(i == 10)
        def _():
            x_last.wait()

        first_layer(i, 0, ps, at(i))
        p_copy(i).start()

        @pl.when(i == 0)
        def _():
            w1_keep.wait()
            for copy in w2_local:
                copy.start()
            for copy in w2_swap:
                copy.start()

    def hidden(i):
        first_layer(i, 1, po, pl.ds(0, M))
        p_copy(i).wait_recv()
        for n in range(half // TILE):
            c = pl.ds(n * TILE, TILE)
            c_in = (po[:, c] + pr[at(i), c]).astype(BF16).astype(F32)
            ho[at(i), c] = gelu_tanh(c_in).astype(BF16)
        h_copy(i).start()

    def second_layer(i):
        @pl.when(i == 0)
        def _():
            for copy in w2_local:
                copy.wait()
            for copy in w2_swap:
                copy.wait_recv()

        for n in range(half // TILE):
            c = pl.ds(n * TILE, TILE)
            zs[at(i), c] = jnp.dot(ho[at(i), :], w2v[0, :, c], preferred_element_type=F32)
        h_copy(i).wait_recv()
        for n in range(half // TILE):
            c = pl.ds(n * TILE, TILE)
            zs[at(i), c] += jnp.dot(hr[at(i), :], w2v[1, :, c], preferred_element_type=F32)

        @pl.when(i == 1)
        def _():
            z_copy(i, 0, 0, partner).start()

        @pl.when((i >= 2) & (i < 5))
        def _():
            z_copy(i, 1, i - 2, along).start()

        @pl.when((i >= 5) & (i < 8))
        def _():
            z_copy(i, 2, i - 5, diagonal).start()

        @pl.when((i >= 8) & (i < 10))
        def _():
            z_copy(i, 0, i - 7, partner).start()

    def step(t, carry):
        @pl.when((t >= 2) & (t < chunks + 2))
        def _():
            hidden(t - 2)

        @pl.when(t < chunks)
        def _():
            partial(t)

        @pl.when(t >= 3)
        def _():
            second_layer(t - 3)

        return carry

    lax.fori_loop(0, chunks + 3, step, 0)

    came = {0: (1, 2, 5), 1: (8, 3, 6), 2: (9, 4, 7)}
    outs = []
    for r in range(per):
        for slot, i in enumerate(came[r]):
            z_copy(i, slot, r, (partner, along, diagonal)[slot]).wait_recv()
        own = pl.ds((0, 10, 11)[r] * M, M)
        row = pl.ds(r * M, M)
        ov[row, :] = (zs[own, :] + zr[0, row, :] + zr[1, row, :] + zr[2, row, :]).astype(BF16)
        outs.append(pltpu.make_async_copy(ov.at[row], z.at[row], out_sem.at[r]))
        outs[-1].start()

    for copy in x_along + x_swap + w2_swap:
        copy.wait_send()
    for k in range(per):
        x_forward(k).wait_send()
    for i in range(chunks):
        p_copy(i).wait_send()
        h_copy(i).wait_send()
    for i in range(1, 10):
        z_copy(i, 0, 0, partner).wait_send()
    for copy in outs:
        copy.wait()


def solution(mesh):
    def body(x, w1, w2):
        rows, half = x.shape
        total, chunks = 4 * rows, 4 * rows // M
        dma = lambda n: pltpu.SemaphoreType.DMA((n,))
        return pl.pallas_call(
            kernel,
            out_shape=jax.ShapeDtypeStruct((rows, half), BF16),
            in_specs=[pl.BlockSpec(memory_space=pl.ANY)] * 3,
            out_specs=pl.BlockSpec(memory_space=pl.ANY),
            scratch_shapes=[
                pltpu.VMEM((total, half), BF16),
                pltpu.VMEM((2, half, half), BF16),
                pltpu.VMEM((2, half, half), BF16),
                pltpu.VMEM((total, half), F32),
                pltpu.VMEM((total, half), F32),
                pltpu.VMEM((M, half), F32),
                pltpu.VMEM((total, half), BF16),
                pltpu.VMEM((total, half), BF16),
                pltpu.VMEM((total, half), F32),
                pltpu.VMEM((3, rows, half), F32),
                pltpu.VMEM((rows, half), BF16),
                dma(2), dma(2), dma(2), dma(3),
                dma(2), dma(2), dma(2), dma(2),
                dma(3), dma(3), dma(3), dma(3),
                dma(chunks), dma(chunks), dma(chunks), dma(chunks), dma(chunks), dma(chunks),
            ],
            compiler_params=pltpu.CompilerParams(
                collective_id=0, has_side_effects=True, vmem_limit_bytes=60 * 1024 * 1024
            ),
        )(x, w1, w2)

    return jax.shard_map(
        body,
        mesh=mesh,
        in_specs=(P(("cx", "cz"), "cy"), P("cy", ("cz", "cx")), P("cz", ("cy", "cx"))),
        out_specs=P(("cx", "cz"), "cy"),
        check_vma=False,
    )
```

time: 338 us -> 164 us (0.49)
  waiting for transfers between devices: 289 us -> 0 us
  Pallas kernels: 0 us -> 162 us
  matrix products: 27.7 us -> 0 us
  between operations: 13.5 us -> 0.01 us
  other arithmetic: 7.37 us -> 0 us
    pallas_call x0 -> x1, Pallas kernels: none -> 162 us  [body(): pl.pallas_call(kernel, out_shape=jax.ShapeDtypeStruct((rows, half), BF16)...]
    all_gather x4 -> x0, waiting for transfers between devices: 146 us -> none  [the longest x1 62.7 us: body(): hg = lax.all_gather(h, 'cy', axis=0, tiled=True)]
    reduce_scatter x2 -> x0, waiting for transfers between devices: 141 us -> none  [the longest x1 108 us: body(): lax.psum_scatter(cp, 'cy', scatter_dimension=0, tiled=True)]
    dot_general x2 -> x0, matrix products: 27.7 us -> none  [the longest x1 13.9 us: body(): zp = jnp.dot(hg, w2g, preferred_element_type=jnp.float32)]
    convert_element_type x2 -> x0, other arithmetic: 7.37 us -> none  [the longest x1 5.23 us: body(): jax.nn.gelu(c.astype(jnp.float32), approximate=True).astype(jnp.bfloat16)]
  transfers between devices with their start and end apart: 6 -> 0, of which waited for: 6 -> 0; matrix products, arithmetic and copies ran while one was open for 2% -> 0% of each run, Pallas kernels for 0% -> 0%
where the time goes in v1:
time: 164 us
  Pallas kernels  162 us (99%)
  local copies, waits for them, and re-layouts  1.92 us (1%)
    pallas_call x1, Pallas kernels, body(): pl.pallas_call(kernel, out_shape=jax.ShapeDtypeStruct((rows, half), BF16)...  162 us

profile of v1, /device:TPU:0, one launch (start us, length us, event | category | flops | bytes accessed | tf_op | source)
XLA Modules:
  0.0 163.7 jit_solution(4616608884599409387)
XLA Ops:
  0.0 161.8 %shard_map.37 = bf16[192,1536]{1,0:T(8,128)(2,1)} custom-call(bf16[192,1536]{1,0:T(8,128)(2,1)} %x.1, bf16[1536,3072]{1,0:T(8,128)(2,1)} %w1.1, bf16[6144,768]{1,0:T(8,128)(2,1)} %w2.1), custom_call_target="tpu_custom_call" | custom-call | tf_op jit(solution)/shard_map/pallas_call | solution.py:219
  161.8 1.9 %copy.5 = bf16[192,1536]{1,0:T(8,128)(2,1)} copy(bf16[192,1536]{1,0:T(8,128)(2,1)} %shard_map.37) | data formatting | bytes 1179648

commit v2 on v1

--- a/solution.py
+++ b/solution.py
@@ -12,14 +12,15 @@
 BF16 = jnp.bfloat16
 M = 64
 TILE = 512
+PIECES = ((0, 512), (512, 512), (1024, 256), (1280, 256))
 
 
 def gelu_tanh(c):
     return 0.5 * c * (1.0 + jnp.tanh(math.sqrt(2 / math.pi) * (c + 0.044715 * (c * c * c))))
 
 
-def kernel(x, w1, w2, z, xv, w1v, w2v, ps, pr, po, ho, hr, zs, zr, ov,
-           xl_sem, w1_sem, w2_sem, out_sem, bx_send, bx_recv, bw_send, bw_recv,
+def kernel(x, w1, w2, z, xv, w1v, w2v, ps, pr, po, ho, hr, zs, zr,
+           xl_sem, w1_sem, w2_sem, bx_send, bx_recv, bw_send, bw_recv,
            xy_send, xy_recv, xf_send, xf_recv, p_send, p_recv, h_send, h_recv, z_send, z_recv):
     cz, cy, cx = lax.axis_index("cz"), lax.axis_index("cy"), lax.axis_index("cx")
     across = {"cy": 1 - cy}
@@ -39,9 +40,14 @@
 
     x_first = pltpu.make_async_copy(x.at[pl.ds(0, M)], xv.at[pl.ds(0, M)], xl_sem.at[0])
     x_last = pltpu.make_async_copy(x.at[pl.ds(M, rows - M)], xv.at[pl.ds(10 * M, rows - M)], xl_sem.at[1])
-    cols = lambda side: pl.ds(pl.multiple_of(side * half, half), half)
-    w1_send = pltpu.make_async_copy(w1.at[:, cols(1 - cy)], w1v.at[0], w1_sem.at[0])
-    w1_keep = pltpu.make_async_copy(w1.at[:, cols(cy)], w1v.at[1], w1_sem.at[1])
+    tiles = half // TILE
+
+    def w1_cols(side, n):
+        return w1.at[:, pl.ds(pl.multiple_of(side * half + n * TILE, TILE), TILE)]
+
+    w1_send = [pltpu.make_async_copy(w1_cols(1 - cy, n), w1v.at[0, :, pl.ds(n * TILE, TILE)], w1_sem.at[n])
+               for n in range(tiles)]
+    w1_keep = pltpu.make_async_copy(w1.at[:, pl.ds(pl.multiple_of(cy * half, half), half)], w1v.at[1], w1_sem.at[tiles])
     width = w2.shape[1]
 
     def w2_rows(core, k):
@@ -70,20 +76,37 @@
     def z_copy(i, slot, row, device):
         return remote(zs.at[at(i)], zr.at[slot, at(row)], z_send.at[i], z_recv.at[i], device)
 
-    x_first.start()
-    w1_send.start()
-    x_last.start()
-    w1_keep.start()
+    def h_piece(k):
+        c = pl.ds(*PIECES[k])
+        return remote(ho.at[at(chunks - 1), c], hr.at[at(chunks - 1), c],
+                      h_send.at[chunks - 1 + k], h_recv.at[chunks - 1 + k], across)
 
     barrier = pltpu.get_barrier_semaphore()
     for device in (across, partner, along, diagonal):
         pl.semaphore_signal(barrier, inc=1, device_id=device, device_id_type=MESH)
+
+    x_first.start()
+    for copy in w1_send:
+        copy.start()
+    x_first.wait()
+    for n in range(tiles):
+        c = pl.ds(n * TILE, TILE)
+        w1_send[n].wait()
+        ps[pl.ds(0, M), c] = jnp.dot(xv[pl.ds(0, M), :], w1v[0, :, c], preferred_element_type=F32)
+    x_last.start()
+    w1_keep.start()
+    for copy in w2_local:
+        copy.start()
+
     pl.semaphore_wait(barrier, 4)
-
+    p_copy(0).start()
+    x_swap[0].start()
     for copy in x_along:
         copy.start()
-    for copy in x_swap:
+    x_swap[1].start()
+    for copy in w2_swap:
         copy.start()
+    w1_keep.wait()
 
     def first_layer(i, side, out, out_rows):
         for n in range(half // TILE):
@@ -91,11 +114,6 @@
             out[out_rows, c] = jnp.dot(xv[at(i), :], w1v[side, :, c], preferred_element_type=F32)
 
     def partial(i):
-        @pl.when(i == 0)
-        def _():
-            x_first.wait()
-            w1_send.wait()
-
         @pl.when(i == 1)
         def _():
             x_swap[0].wait_recv()
@@ -121,22 +139,27 @@
         first_layer(i, 0, ps, at(i))
         p_copy(i).start()
 
-        @pl.when(i == 0)
-        def _():
-            w1_keep.wait()
-            for copy in w2_local:
-                copy.start()
-            for copy in w2_swap:
-                copy.start()
+    def activate(i, c):
+        total = (po[:, c] + pr[at(i), c]).astype(BF16).astype(F32)
+        ho[at(i), c] = gelu_tanh(total).astype(BF16)
 
     def hidden(i):
         first_layer(i, 1, po, pl.ds(0, M))
         p_copy(i).wait_recv()
-        for n in range(half // TILE):
-            c = pl.ds(n * TILE, TILE)
-            c_in = (po[:, c] + pr[at(i), c]).astype(BF16).astype(F32)
-            ho[at(i), c] = gelu_tanh(c_in).astype(BF16)
+        for n in range(tiles):
+            activate(i, pl.ds(n * TILE, TILE))
         h_copy(i).start()
+
+    def second_own(i):
+        for n in range(tiles):
+            c = pl.ds(n * TILE, TILE)
+            zs[at(i), c] = jnp.dot(ho[at(i), :], w2v[0, :, c], preferred_element_type=F32)
+
+    def second_other(i):
+        h_copy(i).wait_recv()
+        for n in range(tiles):
+            c = pl.ds(n * TILE, TILE)
+            zs[at(i), c] += jnp.dot(hr[at(i), :], w2v[1, :, c], preferred_element_type=F32)
 
     def second_layer(i):
         @pl.when(i == 0)
@@ -146,13 +169,8 @@
             for copy in w2_swap:
                 copy.wait_recv()
 
-        for n in range(half // TILE):
-            c = pl.ds(n * TILE, TILE)
-            zs[at(i), c] = jnp.dot(ho[at(i), :], w2v[0, :, c], preferred_element_type=F32)
-        h_copy(i).wait_recv()
-        for n in range(half // TILE):
-            c = pl.ds(n * TILE, TILE)
-            zs[at(i), c] += jnp.dot(hr[at(i), :], w2v[1, :, c], preferred_element_type=F32)
+        second_own(i)
+        second_other(i)
 
         @pl.when(i == 1)
         def _():
@@ -171,7 +189,7 @@
             z_copy(i, 0, i - 7, partner).start()
 
     def step(t, carry):
-        @pl.when((t >= 2) & (t < chunks + 2))
+        @pl.when(t >= 2)
         def _():
             hidden(t - 2)
 
@@ -185,18 +203,47 @@
 
         return carry
 
-    lax.fori_loop(0, chunks + 3, step, 0)
-
-    came = {0: (1, 2, 5), 1: (8, 3, 6), 2: (9, 4, 7)}
-    outs = []
-    for r in range(per):
-        for slot, i in enumerate(came[r]):
+    lax.fori_loop(1, chunks + 1, step, 0)
+
+    last = chunks - 1
+    first_layer(last, 1, po, pl.ds(0, M))
+    p_copy(last).wait_recv()
+    for k, piece in enumerate(PIECES):
+        activate(last, pl.ds(*piece))
+        h_piece(k).start()
+    second_own(last)
+    second_own(last - 1)
+
+    def others(r):
+        came = ((1, 2, 5), (8, 3, 6), (9, 4, 7))[r]
+        for slot, i in enumerate(came):
             z_copy(i, slot, r, (partner, along, diagonal)[slot]).wait_recv()
-        own = pl.ds((0, 10, 11)[r] * M, M)
         row = pl.ds(r * M, M)
-        ov[row, :] = (zs[own, :] + zr[0, row, :] + zr[1, row, :] + zr[2, row, :]).astype(BF16)
-        outs.append(pltpu.make_async_copy(ov.at[row], z.at[row], out_sem.at[r]))
-        outs[-1].start()
+        return row, lambda c: zr[0, row, c] + zr[1, row, c] + zr[2, row, c]
+
+    def finish(r, i):
+        row, came = others(r)
+        for n in range(tiles):
+            c = pl.ds(n * TILE, TILE)
+            z[row, c] = (zs[at(i), c] + came(c)).astype(BF16)
+
+    finish(0, 0)
+    row, came = others(2)
+    for n in range(tiles):
+        c = pl.ds(n * TILE, TILE)
+        zs[at(last), c] += came(c)
+    second_other(last - 1)
+    finish(1, last - 1)
+    for k, (start, width) in enumerate(PIECES):
+        h_piece(k).wait_recv()
+        for n in range(tiles):
+            c = pl.ds(n * TILE, TILE)
+            total = zs[at(last), c] + jnp.dot(
+                hr[at(last), pl.ds(start, width)], w2v[1, pl.ds(start, width), c], preferred_element_type=F32)
+            if k < len(PIECES) - 1:
+                zs[at(last), c] = total
+            else:
+                z[row, c] = total.astype(BF16)
 
     for copy in x_along + x_swap + w2_swap:
         copy.wait_send()
@@ -204,11 +251,12 @@
         x_forward(k).wait_send()
     for i in range(chunks):
         p_copy(i).wait_send()
+    for i in range(chunks - 1):
         h_copy(i).wait_send()
+    for k in range(len(PIECES)):
+        h_piece(k).wait_send()
     for i in range(1, 10):
         z_copy(i, 0, 0, partner).wait_send()
-    for copy in outs:
-        copy.wait()
 
 
 def solution(mesh):
@@ -216,11 +264,12 @@
         rows, half = x.shape
         total, chunks = 4 * rows, 4 * rows // M
         dma = lambda n: pltpu.SemaphoreType.DMA((n,))
+        last = chunks - 1 + len(PIECES)
         return pl.pallas_call(
             kernel,
             out_shape=jax.ShapeDtypeStruct((rows, half), BF16),
             in_specs=[pl.BlockSpec(memory_space=pl.ANY)] * 3,
-            out_specs=pl.BlockSpec(memory_space=pl.ANY),
+            out_specs=pl.BlockSpec(memory_space=pltpu.VMEM),
             scratch_shapes=[
                 pltpu.VMEM((total, half), BF16),
                 pltpu.VMEM((2, half, half), BF16),
@@ -232,16 +281,15 @@
                 pltpu.VMEM((total, half), BF16),
                 pltpu.VMEM((total, half), F32),
                 pltpu.VMEM((3, rows, half), F32),
-                pltpu.VMEM((rows, half), BF16),
-                dma(2), dma(2), dma(2), dma(3),
+                dma(2), dma(half // TILE + 1), dma(2),
                 dma(2), dma(2), dma(2), dma(2),
                 dma(3), dma(3), dma(3), dma(3),
-                dma(chunks), dma(chunks), dma(chunks), dma(chunks), dma(chunks), dma(chunks),
+                dma(chunks), dma(chunks), dma(last), dma(last), dma(chunks), dma(chunks),
             ],
             compiler_params=pltpu.CompilerParams(
-                collective_id=0, has_side_effects=True, vmem_limit_bytes=60 * 1024 * 1024
+                collective_id=0, has_side_effects=True, vmem_limit_bytes=48 * 1024 * 1024
             ),
-        )(x, w1, w2)
+        )(pltpu.with_memory_space_constraint(x, pltpu.HBM), w1, w2)
 
     return jax.shard_map(
         body,

time: 164 us -> 161 us (0.982)
  Pallas kernels: 162 us -> 160 us
    pallas_call x1, Pallas kernels: 162 us -> 160 us  [body(): pl.pallas_call(kernel, out_shape=jax.ShapeDtypeStruct((rows, half), BF16)...]
where the time goes in v2:
time: 161 us
  Pallas kernels  160 us (99%)
    pallas_call x1, Pallas kernels, body(): pl.pallas_call(kernel, out_shape=jax.ShapeDtypeStruct((rows, half), BF16)...  160 us

profile of v2, /device:TPU:0, one launch (start us, length us, event | category | flops | bytes accessed | tf_op | source)
XLA Modules:
  0.0 160.9 jit_solution(12124479805539915662)
XLA Ops:
  0.0 160.0 %shard_map.37 = bf16[192,1536]{1,0:T(8,128)(2,1)S(1)} custom-call(bf16[192,1536]{1,0:T(8,128)(2,1)} %x.1, bf16[1536,3072]{1,0:T(8,128)(2,1)} %w1.1, bf16[6144,768]{1,0:T(8,128)(2,1)} %w2.1), custom_call_target="tpu_custom_call" | custom-call | tf_op jit(solution)/shard_map/pallas_call | solution.py:268
  160.1 0.8 copy.5

commit v3 on v2

--- a/solution.py
+++ b/solution.py
@@ -12,6 +12,7 @@
 BF16 = jnp.bfloat16
 M = 64
 TILE = 512
+FIRST = ((0, 256), (256, 256), (512, 512), (1024, 512))
 PIECES = ((0, 512), (512, 512), (1024, 256), (1280, 256))
 
 
@@ -42,12 +43,14 @@
     x_last = pltpu.make_async_copy(x.at[pl.ds(M, rows - M)], xv.at[pl.ds(10 * M, rows - M)], xl_sem.at[1])
     tiles = half // TILE
 
-    def w1_cols(side, n):
-        return w1.at[:, pl.ds(pl.multiple_of(side * half + n * TILE, TILE), TILE)]
-
-    w1_send = [pltpu.make_async_copy(w1_cols(1 - cy, n), w1v.at[0, :, pl.ds(n * TILE, TILE)], w1_sem.at[n])
-               for n in range(tiles)]
-    w1_keep = pltpu.make_async_copy(w1.at[:, pl.ds(pl.multiple_of(cy * half, half), half)], w1v.at[1], w1_sem.at[tiles])
+    parts = len(FIRST)
+
+    def w1_cols(side, start, width):
+        return w1.at[:, pl.ds(pl.multiple_of(side * half + start, 128), width)]
+
+    w1_send = [pltpu.make_async_copy(w1_cols(1 - cy, *piece), w1v.at[0, :, pl.ds(*piece)], w1_sem.at[k])
+               for k, piece in enumerate(FIRST)]
+    w1_keep = pltpu.make_async_copy(w1_cols(cy, 0, half), w1v.at[1], w1_sem.at[parts])
     width = w2.shape[1]
 
     def w2_rows(core, k):
@@ -76,6 +79,11 @@
     def z_copy(i, slot, row, device):
         return remote(zs.at[at(i)], zr.at[slot, at(row)], z_send.at[i], z_recv.at[i], device)
 
+    def p_piece(k):
+        c = pl.ds(*FIRST[k])
+        sem = k if k == 0 else chunks - 1 + k
+        return remote(ps.at[pl.ds(0, M), c], pr.at[pl.ds(0, M), c], p_send.at[sem], p_recv.at[sem], across)
+
     def h_piece(k):
         c = pl.ds(*PIECES[k])
         return remote(ho.at[at(chunks - 1), c], hr.at[at(chunks - 1), c],
@@ -86,20 +94,24 @@
         pl.semaphore_signal(barrier, inc=1, device_id=device, device_id_type=MESH)
 
     x_first.start()
-    for copy in w1_send:
-        copy.start()
+    w1_send[0].start()
     x_first.wait()
-    for n in range(tiles):
-        c = pl.ds(n * TILE, TILE)
-        w1_send[n].wait()
+    for k in range(parts):
+        c = pl.ds(*FIRST[k])
+        w1_send[k].wait()
+        if k == 0:
+            w1_send[1].start()
+        if k < parts - 2:
+            w1_send[k + 2].start()
         ps[pl.ds(0, M), c] = jnp.dot(xv[pl.ds(0, M), :], w1v[0, :, c], preferred_element_type=F32)
+        if k == 0:
+            pl.semaphore_wait(barrier, 4)
+        p_piece(k).start()
+
     x_last.start()
     w1_keep.start()
     for copy in w2_local:
         copy.start()
-
-    pl.semaphore_wait(barrier, 4)
-    p_copy(0).start()
     x_swap[0].start()
     for copy in x_along:
         copy.start()
@@ -145,7 +157,16 @@
 
     def hidden(i):
         first_layer(i, 1, po, pl.ds(0, M))
-        p_copy(i).wait_recv()
+
+        @pl.when(i == 0)
+        def _():
+            for k in range(parts):
+                p_piece(k).wait_recv()
+
+        @pl.when(i > 0)
+        def _():
+            p_copy(i).wait_recv()
+
         for n in range(tiles):
             activate(i, pl.ds(n * TILE, TILE))
         h_copy(i).start()
@@ -249,7 +270,9 @@
         copy.wait_send()
     for k in range(per):
         x_forward(k).wait_send()
-    for i in range(chunks):
+    for k in range(parts):
+        p_piece(k).wait_send()
+    for i in range(1, chunks):
         p_copy(i).wait_send()
     for i in range(chunks - 1):
         h_copy(i).wait_send()
@@ -264,7 +287,7 @@
         rows, half = x.shape
         total, chunks = 4 * rows, 4 * rows // M
         dma = lambda n: pltpu.SemaphoreType.DMA((n,))
-        last = chunks - 1 + len(PIECES)
+        first, last = chunks - 1 + len(FIRST), chunks - 1 + len(PIECES)
         return pl.pallas_call(
             kernel,
             out_shape=jax.ShapeDtypeStruct((rows, half), BF16),
@@ -281,10 +304,10 @@
                 pltpu.VMEM((total, half), BF16),
                 pltpu.VMEM((total, half), F32),
                 pltpu.VMEM((3, rows, half), F32),
-                dma(2), dma(half // TILE + 1), dma(2),
+                dma(2), dma(len(FIRST) + 1), dma(2),
                 dma(2), dma(2), dma(2), dma(2),
                 dma(3), dma(3), dma(3), dma(3),
-                dma(chunks), dma(chunks), dma(last), dma(last), dma(chunks), dma(chunks),
+                dma(first), dma(first), dma(last), dma(last), dma(chunks), dma(chunks),
             ],
             compiler_params=pltpu.CompilerParams(
                 collective_id=0, has_side_effects=True, vmem_limit_bytes=48 * 1024 * 1024

time: 161 us -> 160 us (level)
  no operation moved by 1% of the time
where the time goes in v3:
time: 160 us
  Pallas kernels  159 us (99%)
    pallas_call x1, Pallas kernels, body(): pl.pallas_call(kernel, out_shape=jax.ShapeDtypeStruct((rows, half), BF16)...  159 us

profile of v3, /device:TPU:0, one launch (start us, length us, event | category | flops | bytes accessed | tf_op | source)
XLA Modules:
  0.0 159.7 jit_solution(8605662470545924594)
XLA Ops:
  0.0 158.8 %shard_map.37 = bf16[192,1536]{1,0:T(8,128)(2,1)S(1)} custom-call(bf16[192,1536]{1,0:T(8,128)(2,1)} %x.1, bf16[1536,3072]{1,0:T(8,128)(2,1)} %w1.1, bf16[6144,768]{1,0:T(8,128)(2,1)} %w2.1), custom_call_target="tpu_custom_call" | custom-call | tf_op jit(solution)/shard_map/pallas_call | solution.py:291
  158.9 0.8 copy.5

commit v4 on v3

--- a/solution.py
+++ b/solution.py
@@ -14,15 +14,16 @@
 TILE = 512
 FIRST = ((0, 256), (256, 256), (512, 512), (1024, 512))
 PIECES = ((0, 512), (512, 512), (1024, 256), (1280, 256))
+DETOUR = 256
 
 
 def gelu_tanh(c):
     return 0.5 * c * (1.0 + jnp.tanh(math.sqrt(2 / math.pi) * (c + 0.044715 * (c * c * c))))
 
 
-def kernel(x, w1, w2, z, xv, w1v, w2v, ps, pr, po, ho, hr, zs, zr,
+def kernel(x, w1, w2, z, xv, w1v, w2v, ps, pr, po, ho, hr, zs, zr, ra, rb, rc,
            xl_sem, w1_sem, w2_sem, bx_send, bx_recv, bw_send, bw_recv,
-           xy_send, xy_recv, xf_send, xf_recv, p_send, p_recv, h_send, h_recv, z_send, z_recv):
+           xy_send, xy_recv, xf_send, xf_recv, p_send, p_recv, h_send, h_recv, z_send, z_recv, r_send, r_recv):
     cz, cy, cx = lax.axis_index("cz"), lax.axis_index("cy"), lax.axis_index("cx")
     across = {"cy": 1 - cy}
     partner = {"cx": 1 - cx}
@@ -38,6 +39,10 @@
 
     def at(i, n=M):
         return pl.ds(pl.multiple_of(i * M, M), n)
+
+    last = chunks - 1
+    detours = (cz == 0) & (cx == 0)
+    relays = (cz == 1) & (cx == 1)
 
     x_first = pltpu.make_async_copy(x.at[pl.ds(0, M)], xv.at[pl.ds(0, M)], xl_sem.at[0])
     x_last = pltpu.make_async_copy(x.at[pl.ds(M, rows - M)], xv.at[pl.ds(10 * M, rows - M)], xl_sem.at[1])
@@ -83,6 +88,18 @@
         c = pl.ds(*FIRST[k])
         sem = k if k == 0 else chunks - 1 + k
         return remote(ps.at[pl.ds(0, M), c], pr.at[pl.ds(0, M), c], p_send.at[sem], p_recv.at[sem], across)
+
+    straight = half - DETOUR
+
+    def p_last():
+        c = pl.ds(0, straight)
+        return remote(ps.at[at(last), c], pr.at[at(last), c], p_send.at[last], p_recv.at[last], across)
+
+    detour = [
+        remote(ra, rb, r_send.at[0], r_recv.at[0], diagonal),
+        remote(rb, rc, r_send.at[1], r_recv.at[1], across),
+        remote(rc, pr.at[at(last), pl.ds(straight, DETOUR)], r_send.at[2], r_recv.at[2], diagonal),
+    ]
 
     def h_piece(k):
         c = pl.ds(*PIECES[k])
@@ -118,6 +135,7 @@
     x_swap[1].start()
     for copy in w2_swap:
         copy.start()
+    x_last.wait()
     w1_keep.wait()
 
     def first_layer(i, side, out, out_rows):
@@ -144,12 +162,15 @@
         def _():
             x_swap[1].wait_recv()
 
-        @pl.when(i == 10)
-        def _():
-            x_last.wait()
-
         first_layer(i, 0, ps, at(i))
-        p_copy(i).start()
+
+        @pl.when(detours & (i == last))
+        def _():
+            p_last().start()
+
+        @pl.when(~(detours & (i == last)))
+        def _():
+            p_copy(i).start()
 
     def activate(i, c):
         total = (po[:, c] + pr[at(i), c]).astype(BF16).astype(F32)
@@ -210,6 +231,21 @@
             z_copy(i, 0, i - 7, partner).start()
 
     def step(t, carry):
+        @pl.when(detours & (t == 3))
+        def _():
+            ra[...] = jnp.dot(xv[at(last), :], w1v[0, :, pl.ds(straight, DETOUR)], preferred_element_type=F32)
+            detour[0].start()
+
+        @pl.when(relays & (t == 4))
+        def _():
+            detour[0].wait_recv()
+            detour[1].start()
+
+        @pl.when(relays & (t == 7))
+        def _():
+            detour[1].wait_recv()
+            detour[2].start()
+
         @pl.when(t >= 2)
         def _():
             hidden(t - 2)
@@ -226,9 +262,17 @@
 
     lax.fori_loop(1, chunks + 1, step, 0)
 
-    last = chunks - 1
     first_layer(last, 1, po, pl.ds(0, M))
-    p_copy(last).wait_recv()
+
+    @pl.when(detours)
+    def _():
+        p_last().wait_recv()
+        detour[2].wait_recv()
+
+    @pl.when(~detours)
+    def _():
+        p_copy(last).wait_recv()
+
     for k, piece in enumerate(PIECES):
         activate(last, pl.ds(*piece))
         h_piece(k).start()
@@ -272,8 +316,23 @@
         x_forward(k).wait_send()
     for k in range(parts):
         p_piece(k).wait_send()
-    for i in range(1, chunks):
+    for i in range(1, last):
         p_copy(i).wait_send()
+
+    @pl.when(detours)
+    def _():
+        p_last().wait_send()
+        detour[0].wait_send()
+
+    @pl.when(~detours)
+    def _():
+        p_copy(last).wait_send()
+
+    @pl.when(relays)
+    def _():
+        detour[1].wait_send()
+        detour[2].wait_send()
+
     for i in range(chunks - 1):
         h_copy(i).wait_send()
     for k in range(len(PIECES)):
@@ -304,10 +363,14 @@
                 pltpu.VMEM((total, half), BF16),
                 pltpu.VMEM((total, half), F32),
                 pltpu.VMEM((3, rows, half), F32),
+                pltpu.VMEM((M, DETOUR), F32),
+                pltpu.VMEM((M, DETOUR), F32),
+                pltpu.VMEM((M, DETOUR), F32),
                 dma(2), dma(len(FIRST) + 1), dma(2),
                 dma(2), dma(2), dma(2), dma(2),
                 dma(3), dma(3), dma(3), dma(3),
                 dma(first), dma(first), dma(last), dma(last), dma(chunks), dma(chunks),
+                dma(3), dma(3),
             ],
             compiler_params=pltpu.CompilerParams(
                 collective_id=0, has_side_effects=True, vmem_limit_bytes=48 * 1024 * 1024

time: 160 us -> 159 us (level)
  no operation moved by 1% of the time
where the time goes in v4:
time: 159 us
  Pallas kernels  158 us (99%)
    pallas_call x1, Pallas kernels, body(): pl.pallas_call(kernel, out_shape=jax.ShapeDtypeStruct((rows, half), BF16)...  158 us

profile of v4, /device:TPU:0, one launch (start us, length us, event | category | flops | bytes accessed | tf_op | source)
XLA Modules:
  0.0 158.8 jit_solution(1264523618183227401)
XLA Ops:
  0.0 158.0 %shard_map.37 = bf16[192,1536]{1,0:T(8,128)(2,1)S(1)} custom-call(bf16[192,1536]{1,0:T(8,128)(2,1)} %x.1, bf16[1536,3072]{1,0:T(8,128)(2,1)} %w1.1, bf16[6144,768]{1,0:T(8,128)(2,1)} %w2.1), custom_call_target="tpu_custom_call" | custom-call | tf_op jit(solution)/shard_map/pallas_call | solution.py:350
  158.0 0.8 copy.5

commit v5 on v4

v5 whole, which is shorter than its diff:
```python
import math

import jax
import jax.numpy as jnp
from jax import lax
from jax.experimental import pallas as pl
from jax.experimental.pallas import tpu as pltpu
from jax.sharding import PartitionSpec as P

MESH = pl.DeviceIdType.MESH
F32 = jnp.float32
BF16 = jnp.bfloat16
M = 64
TILE = 512
FIRST = ((0, 256), (256, 256), (512, 512), (1024, 512))
PIECES = ((0, 768), (768, 512), (1280, 256))
SLOTS = 4
DETOUR = 256


def gelu_tanh(c):
    return 0.5 * c * (1.0 + jnp.tanh(math.sqrt(2 / math.pi) * (c + 0.044715 * (c * c * c))))


def kernel(x, w1, w2, z, xv, w1v, w2v, ps, pr, po, ho, hr, zs, zr, ra, rb, rc,
           xl_sem, w1_sem, w2_sem, bx_send, bx_recv, bw_send, bw_recv,
           xy_send, xy_recv, xf_send, xf_recv, p_send, p_recv, h_send, h_recv, z_send, z_recv, r_send, r_recv):
    cz, cy, cx = lax.axis_index("cz"), lax.axis_index("cy"), lax.axis_index("cx")
    across = {"cy": 1 - cy}
    partner = {"cx": 1 - cx}
    along = {"cz": 1 - cz}
    diagonal = {"cz": 1 - cz, "cx": 1 - cx}
    rows, half = x.shape
    chunks = 4 * rows // M
    per = rows // M

    def remote(src, dst, send, recv, device):
        return pltpu.make_async_remote_copy(src_ref=src, dst_ref=dst, send_sem=send, recv_sem=recv,
                                            device_id=device, device_id_type=MESH)

    def at(i, n=M):
        return pl.ds(pl.multiple_of(i * M, M), n)

    last = chunks - 1
    detours = (cz == 0) & (cx == 0)
    relays = (cz == 1) & (cx == 1)

    x_first = pltpu.make_async_copy(x.at[pl.ds(0, M)], xv.at[pl.ds(0, M)], xl_sem.at[0])
    x_last = pltpu.make_async_copy(x.at[pl.ds(M, rows - M)], xv.at[pl.ds(10 * M, rows - M)], xl_sem.at[0])
    tiles = half // TILE

    def w1_cols(side, start, width):
        return w1.at[:, pl.ds(pl.multiple_of(side * half + start, 128), width)]

    w1_send = [pltpu.make_async_copy(w1_cols(1 - cy, *piece), w1v.at[0, :, pl.ds(*piece)], w1_sem.at[k % 2])
               for k, piece in enumerate(FIRST)]
    w1_keep = pltpu.make_async_copy(w1_cols(cy, 0, half), w1v.at[1], w1_sem.at[0])
    width = w2.shape[1]

    def w2_rows(core, k):
        side = cy if k == 0 else 1 - cy
        return w2.at[pl.ds(pl.multiple_of((core * 2 + side) * half, half), half)]

    mine = pl.ds(pl.multiple_of(cx * width, width), width)
    both = pl.ds(0, 2 * half)
    w2_half = [pl.ds(k * half, half) for k in range(2)]
    w2_local = [pltpu.make_async_copy(w2_rows(cx, k), w2v.at[w2_half[k], mine], w2_sem.at[0]) for k in range(2)]
    w2_local_all = pltpu.make_async_copy(w2.at[both], w2v.at[:, mine], w2_sem.at[0])
    w2_swap = [remote(w2_rows(1 - cx, k), w2v.at[w2_half[k], mine], bw_send.at[0], bw_recv.at[0], partner)
               for k in range(2)]
    w2_swap_all = remote(w2.at[both], w2v.at[:, mine], bw_send.at[0], bw_recv.at[0], partner)
    x_swap = [
        remote(x.at[pl.ds(0, M)], xv.at[pl.ds(M, M)], bx_send.at[0], bx_recv.at[0], partner),
        remote(x.at[pl.ds(M, rows - M)], xv.at[pl.ds(8 * M, rows - M)], bx_send.at[0], bx_recv.at[0], partner),
    ]
    x_swap_all = remote(x, xv.at[pl.ds(7 * M, rows)], bx_send.at[0], bx_recv.at[0], partner)
    x_along = [
        remote(x.at[pl.ds(0, M)], xv.at[pl.ds(2 * M, M)], xy_send.at[0], xy_recv.at[0], along),
        remote(x.at[pl.ds(M, rows - M)], xv.at[pl.ds(3 * M, rows - M)], xy_send.at[0], xy_recv.at[1], along),
    ]
    x_along_all = remote(x, xv.at[pl.ds(2 * M, rows)], xy_send.at[0], xy_recv.at[0], along)
    x_forward = [
        remote(xv.at[pl.ds(2 * M, M)], xv.at[pl.ds(5 * M, M)], xf_send.at[0], xf_recv.at[0], partner),
        remote(xv.at[pl.ds(3 * M, rows - M)], xv.at[pl.ds(6 * M, rows - M)], xf_send.at[0], xf_recv.at[0], partner),
    ]
    x_forward_all = remote(xv.at[pl.ds(2 * M, rows)], xv.at[pl.ds(5 * M, rows)], xf_send.at[0], xf_recv.at[0], partner)

    def p_copy(i):
        return remote(ps.at[at(i)], pr.at[at(i)], p_send.at[0], p_recv.at[i % SLOTS], across)

    def h_copy(i):
        return remote(ho.at[at(i)], hr.at[at(i)], h_send.at[0], h_recv.at[i % SLOTS], across)

    def z_copy(i, slot, row, device):
        return remote(zs.at[at(i)], zr.at[at(slot * per + row)], z_send.at[0], z_recv.at[0], device)

    z_all = remote(zs.at[pl.ds(0, 3 * rows)], zr, z_send.at[0], z_recv.at[0], partner)
    parts = len(FIRST)

    def p_piece(k):
        c = pl.ds(*FIRST[k])
        return remote(ps.at[pl.ds(0, M), c], pr.at[pl.ds(0, M), c], p_send.at[0], p_recv.at[0], across)

    straight = half - DETOUR

    def p_last():
        c = pl.ds(0, straight)
        return remote(ps.at[at(last), c], pr.at[at(last), c], p_send.at[1], p_recv.at[last % SLOTS], across)

    def p_whole():
        return remote(ps.at[at(last)], pr.at[at(last)], p_send.at[1], p_recv.at[last % SLOTS], across)

    detour = [
        remote(ra, rb, r_send.at[0], r_recv.at[0], diagonal),
        remote(rb, rc, r_send.at[0], r_recv.at[1], across),
        remote(rc, pr.at[at(last), pl.ds(straight, DETOUR)], r_send.at[0], r_recv.at[0], diagonal),
    ]

    def h_piece(k):
        c = pl.ds(*PIECES[k])
        return remote(ho.at[at(chunks - 1), c], hr.at[at(chunks - 1), c],
                      h_send.at[0], h_recv.at[SLOTS + k], across)

    barrier = pltpu.get_barrier_semaphore()
    for device in (across, partner, along, diagonal):
        pl.semaphore_signal(barrier, inc=1, device_id=device, device_id_type=MESH)

    x_first.start()
    w1_send[0].start()
    x_first.wait()
    for k in range(parts):
        c = pl.ds(*FIRST[k])
        w1_send[k].wait()
        if k == 0:
            w1_send[1].start()
        if k < parts - 2:
            w1_send[k + 2].start()
        ps[pl.ds(0, M), c] = jnp.dot(xv[pl.ds(0, M), :], w1v[0, :, c], preferred_element_type=F32)
        if k == 0:
            pl.semaphore_wait(barrier, 4)
        p_piece(k).start()

    x_last.start()
    w1_keep.start()
    for copy in w2_local:
        copy.start()
    x_swap[0].start()
    for copy in x_along:
        copy.start()
    x_swap[1].start()
    for copy in w2_swap:
        copy.start()
    x_last.wait()
    w1_keep.wait()

    def first_layer(i, side, out, out_rows):
        for n in range(half // TILE):
            c = pl.ds(n * TILE, TILE)
            out[out_rows, c] = jnp.dot(xv[at(i), :], w1v[side, :, c], preferred_element_type=F32)

    def partial(i):
        @pl.when(i == 1)
        def _():
            x_swap_all.wait_recv()

        for k in range(2):
            @pl.when(i == 2 + k)
            def _():
                x_along[k].wait_recv()
                x_forward[k].start()

        @pl.when(i == 5)
        def _():
            x_forward_all.wait_recv()

        first_layer(i, 0, ps, at(i))

        @pl.when(detours & (i == last))
        def _():
            p_last().start()

        @pl.when(~detours & (i == last))
        def _():
            p_whole().start()

        @pl.when(i < last)
        def _():
            p_copy(i).start()

    def activate(i, c):
        total = (po[:, c] + pr[at(i), c]).astype(BF16).astype(F32)
        ho[at(i), c] = gelu_tanh(total).astype(BF16)

    def hidden(i):
        first_layer(i, 1, po, pl.ds(0, M))
        p_copy(i).wait_recv()
        for n in range(tiles):
            activate(i, pl.ds(n * TILE, TILE))
        h_copy(i).start()

    def second_own(i):
        for n in range(tiles):
            c = pl.ds(n * TILE, TILE)
            zs[at(i), c] = jnp.dot(ho[at(i), :], w2v[w2_half[0], c], preferred_element_type=F32)

    def second_other(i):
        h_copy(i).wait_recv()
        for n in range(tiles):
            c = pl.ds(n * TILE, TILE)
            zs[at(i), c] += jnp.dot(hr[at(i), :], w2v[w2_half[1], c], preferred_element_type=F32)

    def second_layer(i):
        @pl.when(i == 0)
        def _():
            w2_local_all.wait()
            w2_swap_all.wait_recv()

        second_own(i)
        second_other(i)

        @pl.when(i == 1)
        def _():
            z_copy(i, 0, 0, partner).start()

        @pl.when((i >= 2) & (i < 5))
        def _():
            z_copy(i, 1, i - 2, along).start()

        @pl.when((i >= 5) & (i < 8))
        def _():
            z_copy(i, 2, i - 5, diagonal).start()

        @pl.when((i >= 8) & (i < 10))
        def _():
            z_copy(i, 0, i - 7, partner).start()

    def step(t, carry):
        @pl.when(detours & (t == 3))
        def _():
            ra[...] = jnp.dot(xv[at(last), :], w1v[0, :, pl.ds(straight, DETOUR)], preferred_element_type=F32)
            detour[0].start()

        @pl.when(relays & (t == 4))
        def _():
            detour[0].wait_recv()
            detour[1].start()

        @pl.when(relays & (t == 7))
        def _():
            detour[1].wait_recv()
            detour[1].wait_send()
            detour[2].start()

        @pl.when(t >= 2)
        def _():
            hidden(t - 2)

        @pl.when(t < chunks)
        def _():
            partial(t)

        @pl.when(t >= 3)
        def _():
            second_layer(t - 3)

        return carry

    lax.fori_loop(1, chunks + 1, step, 0)

    first_layer(last, 1, po, pl.ds(0, M))

    @pl.when(detours)
    def _():
        p_last().wait_recv()
        detour[2].wait_recv()

    @pl.when(~detours)
    def _():
        p_whole().wait_recv()

    for k, piece in enumerate(PIECES):
        activate(last, pl.ds(*piece))
        h_piece(k).start()
    second_own(last)
    second_own(last - 1)

    z_all.wait_recv()

    def came(r, c):
        return zr[pl.ds(r * M, M), c] + zr[pl.ds(rows + r * M, M), c] + zr[pl.ds(2 * rows + r * M, M), c]

    def finish(r, i):
        for n in range(tiles):
            c = pl.ds(n * TILE, TILE)
            z[pl.ds(r * M, M), c] = (zs[at(i), c] + came(r, c)).astype(BF16)

    finish(0, 0)
    for n in range(tiles):
        c = pl.ds(n * TILE, TILE)
        zs[at(last), c] += came(2, c)
    second_other(last - 1)
    finish(1, last - 1)
    for k, (start, width) in enumerate(PIECES):
        h_piece(k).wait_recv()
        for n in range(tiles):
            c = pl.ds(n * TILE, TILE)
            total = zs[at(last), c] + jnp.dot(
                hr[at(last), pl.ds(start, width)], w2v[pl.ds(half + start, width), c], preferred_element_type=F32)
            if k < len(PIECES) - 1:
                zs[at(last), c] = total
            else:
                z[pl.ds(2 * M, M), c] = total.astype(BF16)

    for copy in (x_along_all, x_swap_all, w2_swap_all, x_forward_all, z_all):
        copy.wait_send()
    most = pl.ds(0, last * M)
    remote(ps.at[most], pr.at[most], p_send.at[0], p_recv.at[0], across).wait_send()
    remote(ho, hr, h_send.at[0], h_recv.at[0], across).wait_send()

    @pl.when(detours)
    def _():
        p_last().wait_send()
        detour[0].wait_send()

    @pl.when(~detours)
    def _():
        p_whole().wait_send()

    @pl.when(relays)
    def _():
        detour[2].wait_send()


def solution(mesh):
    def body(x, w1, w2):
        rows, half = x.shape
        total = 4 * rows
        dma = lambda n: pltpu.SemaphoreType.DMA((n,))
        return pl.pallas_call(
            kernel,
            out_shape=jax.ShapeDtypeStruct((rows, half), BF16),
            in_specs=[pl.BlockSpec(memory_space=pl.ANY)] * 3,
            out_specs=pl.BlockSpec(memory_space=pltpu.VMEM),
            scratch_shapes=[
                pltpu.VMEM((total, half), BF16),
                pltpu.VMEM((2, half, half), BF16),
                pltpu.VMEM((2 * half, half), BF16),
                pltpu.VMEM((total, half), F32),
                pltpu.VMEM((total, half), F32),
                pltpu.VMEM((M, half), F32),
                pltpu.VMEM((total, half), BF16),
                pltpu.VMEM((total, half), BF16),
                pltpu.VMEM((total, half), F32),
                pltpu.VMEM((3 * rows, half), F32),
                pltpu.VMEM((M, DETOUR), F32),
                pltpu.VMEM((M, DETOUR), F32),
                pltpu.VMEM((M, DETOUR), F32),
                dma(1), dma(2), dma(1),
                dma(1), dma(1), dma(1), dma(1),
                dma(1), dma(2), dma(1), dma(1),
                dma(2), dma(SLOTS), dma(1), dma(SLOTS + len(PIECES)),
                dma(1), dma(1), dma(1), dma(2),
            ],
            compiler_params=pltpu.CompilerParams(
                collective_id=0, has_side_effects=True, vmem_limit_bytes=48 * 1024 * 1024
            ),
        )(pltpu.with_memory_space_constraint(x, pltpu.HBM), w1, w2)

    return jax.shard_map(
        body,
        mesh=mesh,
        in_specs=(P(("cx", "cz"), "cy"), P("cy", ("cz", "cx")), P("cz", ("cy", "cx"))),
        out_specs=P(("cx", "cz"), "cy"),
        check_vma=False,
    )
```

time: 159 us -> 158 us (level)
  no operation moved by 1% of the time
where the time goes in v5:
time: 158 us
  Pallas kernels  157 us (99%)
    pallas_call x1, Pallas kernels, body(): pl.pallas_call(kernel, out_shape=jax.ShapeDtypeStruct((rows, half), BF16)...  157 us

profile of v5, /device:TPU:0, one launch (start us, length us, event | category | flops | bytes accessed | tf_op | source)
XLA Modules:
  0.0 158.0 jit_solution(524073294523143162)
XLA Ops:
  0.0 157.1 %shard_map.37 = bf16[192,1536]{1,0:T(8,128)(2,1)S(1)} custom-call(bf16[192,1536]{1,0:T(8,128)(2,1)} %x.1, bf16[1536,3072]{1,0:T(8,128)(2,1)} %w1.1, bf16[6144,768]{1,0:T(8,128)(2,1)} %w2.1), custom_call_target="tpu_custom_call" | custom-call | tf_op jit(solution)/shard_map/pallas_call | solution.py:339
  157.1 0.8 copy.5

commit v6 on v5

--- a/solution.py
+++ b/solution.py
@@ -13,7 +13,9 @@
 M = 64
 TILE = 512
 FIRST = ((0, 256), (256, 256), (512, 512), (1024, 512))
-PIECES = ((0, 768), (768, 512), (1280, 256))
+SKEW = 256
+TO_LOW = ((0, 768), (768, 512), (1280, 256))
+TO_HIGH = ((0, 768), (768, 256), (1024, 256))
 SLOTS = 4
 DETOUR = 256
 
@@ -22,7 +24,7 @@
     return 0.5 * c * (1.0 + jnp.tanh(math.sqrt(2 / math.pi) * (c + 0.044715 * (c * c * c))))
 
 
-def kernel(x, w1, w2, z, xv, w1v, w2v, ps, pr, po, ho, hr, zs, zr, ra, rb, rc,
+def kernel(x, w1, w2, z, xv, w1v, w2v, ps, pr, po, ho, hr, zs, zr, ra, rb, rc, pe, pq,
            xl_sem, w1_sem, w2_sem, bx_send, bx_recv, bw_send, bw_recv,
            xy_send, xy_recv, xf_send, xf_recv, p_send, p_recv, h_send, h_recv, z_send, z_recv, r_send, r_recv):
     cz, cy, cx = lax.axis_index("cz"), lax.axis_index("cy"), lax.axis_index("cx")
@@ -42,6 +44,8 @@
         return pl.ds(pl.multiple_of(i * M, M), n)
 
     last = chunks - 1
+    low, high = cy == 0, cy == 1
+    kept = half - SKEW
     detours = (cz == 0) & (cx == 0)
     relays = (cz == 1) & (cx == 1)
 
@@ -103,23 +107,36 @@
 
     straight = half - DETOUR
 
-    def p_last():
+    def p_straight():
         c = pl.ds(0, straight)
-        return remote(ps.at[at(last), c], pr.at[at(last), c], p_send.at[1], p_recv.at[last % SLOTS], across)
+        return remote(ps.at[at(last - 1), c], pr.at[at(last - 1), c], p_send.at[1], p_recv.at[(last - 1) % SLOTS], across)
 
     def p_whole():
-        return remote(ps.at[at(last)], pr.at[at(last)], p_send.at[1], p_recv.at[last % SLOTS], across)
+        return remote(ps.at[at(last - 1)], pr.at[at(last - 1)], p_send.at[1], p_recv.at[(last - 1) % SLOTS], across)
+
+    def p_high():
+        return remote(ps.at[at(last)], pr.at[at(last)], p_send.at[2], p_recv.at[last % SLOTS], across)
+
+    def p_over():
+        return remote(pe, pq, p_send.at[3], p_recv.at[SLOTS], across)
+
+    def p_low():
+        c = pl.ds(0, kept)
+        return remote(ps.at[at(last), c], pr.at[at(last), c], p_send.at[2], p_recv.at[last % SLOTS], across)
 
     detour = [
         remote(ra, rb, r_send.at[0], r_recv.at[0], diagonal),
         remote(rb, rc, r_send.at[0], r_recv.at[1], across),
-        remote(rc, pr.at[at(last), pl.ds(straight, DETOUR)], r_send.at[0], r_recv.at[0], diagonal),
+        remote(rc, pr.at[at(last - 1), pl.ds(straight, DETOUR)], r_send.at[0], r_recv.at[0], diagonal),
     ]
 
-    def h_piece(k):
-        c = pl.ds(*PIECES[k])
-        return remote(ho.at[at(chunks - 1), c], hr.at[at(chunks - 1), c],
-                      h_send.at[0], h_recv.at[SLOTS + k], across)
+    def h_piece(k, piece):
+        c = pl.ds(*piece)
+        return remote(ho.at[at(last), c], hr.at[at(last), c], h_send.at[1], h_recv.at[SLOTS + k], across)
+
+    def h_over():
+        c = pl.ds(kept, SKEW)
+        return remote(hr.at[at(last), c], ho.at[at(last), c], h_send.at[2], h_recv.at[SLOTS + len(TO_LOW)], across)
 
     barrier = pltpu.get_barrier_semaphore()
     for device in (across, partner, along, diagonal):
@@ -173,19 +190,32 @@
         def _():
             x_forward_all.wait_recv()
 
+        @pl.when(low & (i == last))
+        def _():
+            pe[...] = jnp.dot(xv[at(last), :], w1v[1, :, pl.ds(kept, SKEW)], preferred_element_type=F32)
+            p_over().start()
+
         first_layer(i, 0, ps, at(i))
 
-        @pl.when(detours & (i == last))
-        def _():
-            p_last().start()
-
-        @pl.when(~detours & (i == last))
+        @pl.when(i < last - 1)
+        def _():
+            p_copy(i).start()
+
+        @pl.when(detours & (i == last - 1))
+        def _():
+            p_straight().start()
+
+        @pl.when(~detours & (i == last - 1))
         def _():
             p_whole().start()
 
-        @pl.when(i < last)
-        def _():
-            p_copy(i).start()
+        @pl.when(low & (i == last))
+        def _():
+            p_high().start()
+
+        @pl.when(high & (i == last))
+        def _():
+            p_low().start()
 
     def activate(i, c):
         total = (po[:, c] + pr[at(i), c]).astype(BF16).astype(F32)
@@ -193,7 +223,16 @@
 
     def hidden(i):
         first_layer(i, 1, po, pl.ds(0, M))
-        p_copy(i).wait_recv()
+
+        @pl.when(~detours | (i < last - 1))
+        def _():
+            p_copy(i).wait_recv()
+
+        @pl.when(detours & (i == last - 1))
+        def _():
+            p_straight().wait_recv()
+            detour[2].wait_recv()
+
         for n in range(tiles):
             activate(i, pl.ds(n * TILE, TILE))
         h_copy(i).start()
@@ -237,7 +276,7 @@
     def step(t, carry):
         @pl.when(detours & (t == 3))
         def _():
-            ra[...] = jnp.dot(xv[at(last), :], w1v[0, :, pl.ds(straight, DETOUR)], preferred_element_type=F32)
+            ra[...] = jnp.dot(xv[at(last - 1), :], w1v[0, :, pl.ds(straight, DETOUR)], preferred_element_type=F32)
             detour[0].start()
 
         @pl.when(relays & (t == 4))
@@ -269,19 +308,48 @@
 
     first_layer(last, 1, po, pl.ds(0, M))
 
-    @pl.when(detours)
-    def _():
-        p_last().wait_recv()
-        detour[2].wait_recv()
-
-    @pl.when(~detours)
-    def _():
-        p_whole().wait_recv()
-
-    for k, piece in enumerate(PIECES):
-        activate(last, pl.ds(*piece))
-        h_piece(k).start()
-    second_own(last)
+    @pl.when(low)
+    def _():
+        p_low().wait_recv()
+        for k, piece in enumerate(TO_HIGH):
+            activate(last, pl.ds(*piece))
+            h_piece(k, piece).start()
+
+    over = pl.ds(kept, SKEW)
+
+    @pl.when(high)
+    def _():
+        p_over().wait_recv()
+        total = (ps[at(last), over] + pq[...]).astype(BF16).astype(F32)
+        hr[at(last), over] = gelu_tanh(total).astype(BF16)
+        h_over().start()
+        p_high().wait_recv()
+        for k, piece in enumerate(TO_LOW):
+            activate(last, pl.ds(*piece))
+            h_piece(k, piece).start()
+
+    def multiply(h, start, width, below, out):
+        for n in range(tiles):
+            c = pl.ds(n * TILE, TILE)
+            out(c, jnp.dot(h[at(last), pl.ds(start, width)], w2v[pl.ds(below + start, width), c],
+                           preferred_element_type=F32))
+
+    def put(c, term):
+        zs[at(last), c] = term
+
+    def add(c, term):
+        zs[at(last), c] += term
+
+    def close(c, term):
+        z[pl.ds(2 * M, M), c] = (zs[at(last), c] + term).astype(BF16)
+
+    multiply(ho, 0, kept, 0, put)
+
+    @pl.when(high)
+    def _():
+        multiply(ho, kept, SKEW, 0, add)
+        multiply(hr, kept, SKEW, half, add)
+
     second_own(last - 1)
 
     z_all.wait_recv()
@@ -300,31 +368,49 @@
         zs[at(last), c] += came(2, c)
     second_other(last - 1)
     finish(1, last - 1)
-    for k, (start, width) in enumerate(PIECES):
-        h_piece(k).wait_recv()
-        for n in range(tiles):
-            c = pl.ds(n * TILE, TILE)
-            total = zs[at(last), c] + jnp.dot(
-                hr[at(last), pl.ds(start, width)], w2v[pl.ds(half + start, width), c], preferred_element_type=F32)
-            if k < len(PIECES) - 1:
-                zs[at(last), c] = total
-            else:
-                z[pl.ds(2 * M, M), c] = total.astype(BF16)
+
+    def close_pieces(pieces):
+        for k, piece in enumerate(pieces):
+            h_piece(k, piece).wait_recv()
+            multiply(hr, *piece, half, add if k < len(pieces) - 1 else close)
+
+    @pl.when(low)
+    def _():
+        h_over().wait_recv()
+        multiply(ho, kept, SKEW, 0, add)
+        close_pieces(TO_LOW)
+
+    @pl.when(high)
+    def _():
+        close_pieces(TO_HIGH)
 
     for copy in (x_along_all, x_swap_all, w2_swap_all, x_forward_all, z_all):
         copy.wait_send()
+    most = pl.ds(0, (last - 1) * M)
+    remote(ps.at[most], pr.at[most], p_send.at[0], p_recv.at[0], across).wait_send()
     most = pl.ds(0, last * M)
-    remote(ps.at[most], pr.at[most], p_send.at[0], p_recv.at[0], across).wait_send()
-    remote(ho, hr, h_send.at[0], h_recv.at[0], across).wait_send()
+    remote(ho.at[most], hr.at[most], h_send.at[0], h_recv.at[0], across).wait_send()
 
     @pl.when(detours)
     def _():
-        p_last().wait_send()
+        p_straight().wait_send()
         detour[0].wait_send()
 
     @pl.when(~detours)
     def _():
         p_whole().wait_send()
+
+    @pl.when(low)
+    def _():
+        p_high().wait_send()
+        p_over().wait_send()
+        h_piece(0, (0, kept)).wait_send()
+
+    @pl.when(high)
+    def _():
+        p_low().wait_send()
+        h_over().wait_send()
+        h_piece(0, (0, half)).wait_send()
 
     @pl.when(relays)
     def _():
@@ -355,10 +441,12 @@
                 pltpu.VMEM((M, DETOUR), F32),
                 pltpu.VMEM((M, DETOUR), F32),
                 pltpu.VMEM((M, DETOUR), F32),
+                pltpu.VMEM((M, SKEW), F32),
+                pltpu.VMEM((M, SKEW), F32),
                 dma(1), dma(2), dma(1),
                 dma(1), dma(1), dma(1), dma(1),
                 dma(1), dma(2), dma(1), dma(1),
-                dma(2), dma(SLOTS), dma(1), dma(SLOTS + len(PIECES)),
+                dma(4), dma(SLOTS + 1), dma(3), dma(SLOTS + len(TO_LOW) + 1),
                 dma(1), dma(1), dma(1), dma(2),
             ],
             compiler_params=pltpu.CompilerParams(

time: 158 us -> 158 us (level)
  no operation moved by 1% of the time
where the time goes in v6:
time: 158 us; the launch traced here: 157 us
  Pallas kernels  157 us (99%)
    pallas_call x1, Pallas kernels, body(): pl.pallas_call(kernel, out_shape=jax.ShapeDtypeStruct((rows, half), BF16)...  157 us

profile of v6, /device:TPU:0, one launch (start us, length us, event | category | flops | bytes accessed | tf_op | source)
XLA Modules:
  0.0 157.5 jit_solution(17010893157436642412)
XLA Ops:
  0.0 156.6 %shard_map.37 = bf16[192,1536]{1,0:T(8,128)(2,1)S(1)} custom-call(bf16[192,1536]{1,0:T(8,128)(2,1)} %x.1, bf16[1536,3072]{1,0:T(8,128)(2,1)} %w1.1, bf16[6144,768]{1,0:T(8,128)(2,1)} %w2.1), custom_call_target="tpu_custom_call" | custom-call | tf_op jit(solution)/shard_map/pallas_call | solution.py:425
  156.6 0.8 copy.5

commit v7 on v6

--- a/solution.py
+++ b/solution.py
@@ -46,8 +46,8 @@
     last = chunks - 1
     low, high = cy == 0, cy == 1
     kept = half - SKEW
-    detours = (cz == 0) & (cx == 0)
-    relays = (cz == 1) & (cx == 1)
+    source, sink = (cz == 0) & (cx == 0) & high, (cz == 0) & (cx == 0) & low
+    relay_high, relay_low = (cz == 1) & (cx == 0) & high, (cz == 1) & (cx == 0) & low
 
     x_first = pltpu.make_async_copy(x.at[pl.ds(0, M)], xv.at[pl.ds(0, M)], xl_sem.at[0])
     x_last = pltpu.make_async_copy(x.at[pl.ds(M, rows - M)], xv.at[pl.ds(10 * M, rows - M)], xl_sem.at[0])
@@ -125,9 +125,9 @@
         return remote(ps.at[at(last), c], pr.at[at(last), c], p_send.at[2], p_recv.at[last % SLOTS], across)
 
     detour = [
-        remote(ra, rb, r_send.at[0], r_recv.at[0], diagonal),
-        remote(rb, rc, r_send.at[0], r_recv.at[1], across),
-        remote(rc, pr.at[at(last - 1), pl.ds(straight, DETOUR)], r_send.at[0], r_recv.at[0], diagonal),
+        remote(ra, rb, r_send.at[0], r_recv.at[0], along),
+        remote(rb, rc, r_send.at[0], r_recv.at[0], across),
+        remote(rc, pr.at[at(last - 1), pl.ds(straight, DETOUR)], r_send.at[0], r_recv.at[0], along),
     ]
 
     def h_piece(k, piece):
@@ -201,11 +201,11 @@
         def _():
             p_copy(i).start()
 
-        @pl.when(detours & (i == last - 1))
+        @pl.when(source & (i == last - 1))
         def _():
             p_straight().start()
 
-        @pl.when(~detours & (i == last - 1))
+        @pl.when(~source & (i == last - 1))
         def _():
             p_whole().start()
 
@@ -224,11 +224,11 @@
     def hidden(i):
         first_layer(i, 1, po, pl.ds(0, M))
 
-        @pl.when(~detours | (i < last - 1))
+        @pl.when(~sink | (i < last - 1))
         def _():
             p_copy(i).wait_recv()
 
-        @pl.when(detours & (i == last - 1))
+        @pl.when(sink & (i == last - 1))
         def _():
             p_straight().wait_recv()
             detour[2].wait_recv()
@@ -249,12 +249,6 @@
             zs[at(i), c] += jnp.dot(hr[at(i), :], w2v[w2_half[1], c], preferred_element_type=F32)
 
     def second_layer(i):
-        @pl.when(i == 0)
-        def _():
-            w2_local_all.wait()
-            w2_swap_all.wait_recv()
-
-        second_own(i)
         second_other(i)
 
         @pl.when(i == 1)
@@ -272,61 +266,6 @@
         @pl.when((i >= 8) & (i < 10))
         def _():
             z_copy(i, 0, i - 7, partner).start()
-
-    def step(t, carry):
-        @pl.when(detours & (t == 3))
-        def _():
-            ra[...] = jnp.dot(xv[at(last - 1), :], w1v[0, :, pl.ds(straight, DETOUR)], preferred_element_type=F32)
-            detour[0].start()
-
-        @pl.when(relays & (t == 4))
-        def _():
-            detour[0].wait_recv()
-            detour[1].start()
-
-        @pl.when(relays & (t == 7))
-        def _():
-            detour[1].wait_recv()
-            detour[1].wait_send()
-            detour[2].start()
-
-        @pl.when(t >= 2)
-        def _():
-            hidden(t - 2)
-
-        @pl.when(t < chunks)
-        def _():
-            partial(t)
-
-        @pl.when(t >= 3)
-        def _():
-            second_layer(t - 3)
-
-        return carry
-
-    lax.fori_loop(1, chunks + 1, step, 0)
-
-    first_layer(last, 1, po, pl.ds(0, M))
-
-    @pl.when(low)
-    def _():
-        p_low().wait_recv()
-        for k, piece in enumerate(TO_HIGH):
-            activate(last, pl.ds(*piece))
-            h_piece(k, piece).start()
-
-    over = pl.ds(kept, SKEW)
-
-    @pl.when(high)
-    def _():
-        p_over().wait_recv()
-        total = (ps[at(last), over] + pq[...]).astype(BF16).astype(F32)
-        hr[at(last), over] = gelu_tanh(total).astype(BF16)
-        h_over().start()
-        p_high().wait_recv()
-        for k, piece in enumerate(TO_LOW):
-            activate(last, pl.ds(*piece))
-            h_piece(k, piece).start()
 
     def multiply(h, start, width, below, out):
         for n in range(tiles):
@@ -340,17 +279,88 @@
     def add(c, term):
         zs[at(last), c] += term
 
+    over = pl.ds(kept, SKEW)
+
+    def hidden_last():
+        first_layer(last, 1, po, pl.ds(0, M))
+
+        @pl.when(low)
+        def _():
+            p_low().wait_recv()
+            for k, piece in enumerate(TO_HIGH):
+                activate(last, pl.ds(*piece))
+                h_piece(k, piece).start()
+
+        @pl.when(high)
+        def _():
+            p_over().wait_recv()
+            total = (ps[at(last), over] + pq[...]).astype(BF16).astype(F32)
+            hr[at(last), over] = gelu_tanh(total).astype(BF16)
+            h_over().start()
+            p_high().wait_recv()
+            for k, piece in enumerate(TO_LOW):
+                activate(last, pl.ds(*piece))
+                h_piece(k, piece).start()
+
+    def own_last():
+        multiply(ho, 0, kept, 0, put)
+
+        @pl.when(high)
+        def _():
+            multiply(ho, kept, SKEW, 0, add)
+            multiply(hr, kept, SKEW, half, add)
+
+    def step(t, carry):
+        @pl.when(source & (t == 3))
+        def _():
+            ra[...] = jnp.dot(xv[at(last - 1), :], w1v[0, :, pl.ds(straight, DETOUR)], preferred_element_type=F32)
+            detour[0].start()
+
+        @pl.when(relay_high & (t == 4))
+        def _():
+            detour[0].wait_recv()
+            detour[1].start()
+
+        @pl.when(relay_low & (t == 7))
+        def _():
+            detour[1].wait_recv()
+            detour[2].start()
+
+        @pl.when(t < chunks)
+        def _():
+            partial(t)
+
+        @pl.when(t >= 2)
+        def _():
+            hidden(t - 2)
+
+        @pl.when(t == chunks)
+        def _():
+            hidden_last()
+
+        @pl.when(t == 2)
+        def _():
+            w2_local_all.wait()
+            w2_swap_all.wait_recv()
+
+        @pl.when(t >= 2)
+        def _():
+            second_own(t - 2)
+
+        @pl.when(t == chunks)
+        def _():
+            own_last()
+
+        @pl.when(t >= 3)
+        def _():
+            second_layer(t - 3)
+
+        return carry
+
+    lax.fori_loop(1, chunks + 1, step, 0)
+
     def close(c, term):
         z[pl.ds(2 * M, M), c] = (zs[at(last), c] + term).astype(BF16)
-
-    multiply(ho, 0, kept, 0, put)
-
-    @pl.when(high)
-    def _():
-        multiply(ho, kept, SKEW, 0, add)
-        multiply(hr, kept, SKEW, half, add)
-
-    second_own(last - 1)
 
     z_all.wait_recv()
 
@@ -391,12 +401,12 @@
     most = pl.ds(0, last * M)
     remote(ho.at[most], hr.at[most], h_send.at[0], h_recv.at[0], across).wait_send()
 
-    @pl.when(detours)
+    @pl.when(source)
     def _():
         p_straight().wait_send()
         detour[0].wait_send()
 
-    @pl.when(~detours)
+    @pl.when(~source)
     def _():
         p_whole().wait_send()
 
@@ -412,7 +422,11 @@
         h_over().wait_send()
         h_piece(0, (0, half)).wait_send()
 
-    @pl.when(relays)
+    @pl.when(relay_high)
+    def _():
+        detour[1].wait_send()
+
+    @pl.when(relay_low)
     def _():
         detour[2].wait_send()
 
@@ -447,7 +461,7 @@
                 dma(1), dma(1), dma(1), dma(1),
                 dma(1), dma(2), dma(1), dma(1),
                 dma(4), dma(SLOTS + 1), dma(3), dma(SLOTS + len(TO_LOW) + 1),
-                dma(1), dma(1), dma(1), dma(2),
+                dma(1), dma(1), dma(1), dma(1),
             ],
             compiler_params=pltpu.CompilerParams(
                 collective_id=0, has_side_effects=True, vmem_limit_bytes=48 * 1024 * 1024

time: 158 us -> 158 us (level)
  no operation moved by 1% of the time
where the time goes in v7:
time: 158 us; the launch traced here: 157 us
  Pallas kernels  157 us (99%)
    pallas_call x1, Pallas kernels, body(): pl.pallas_call(kernel, out_shape=jax.ShapeDtypeStruct((rows, half), BF16)...  157 us

profile of v7, /device:TPU:0, one launch (start us, length us, event | category | flops | bytes accessed | tf_op | source)
XLA Modules:
  0.0 157.4 jit_solution(13920202834373710003)
XLA Ops:
  0.0 156.6 %shard_map.37 = bf16[192,1536]{1,0:T(8,128)(2,1)S(1)} custom-call(bf16[192,1536]{1,0:T(8,128)(2,1)} %x.1, bf16[1536,3072]{1,0:T(8,128)(2,1)} %w1.1, bf16[6144,768]{1,0:T(8,128)(2,1)} %w2.1), custom_call_target="tpu_custom_call" | custom-call | tf_op jit(solution)/shard_map/pallas_call | solution.py:439
  156.6 0.8 copy.5

commit v8 on v7

--- a/solution.py
+++ b/solution.py
@@ -12,12 +12,12 @@
 BF16 = jnp.bfloat16
 M = 64
 TILE = 512
-FIRST = ((0, 256), (256, 256), (512, 512), (1024, 512))
+FIRST = ((0, 128), (128, 256), (384, 384), (768, 768))
 SKEW = 256
 TO_LOW = ((0, 768), (768, 512), (1280, 256))
 TO_HIGH = ((0, 768), (768, 256), (1024, 256))
 SLOTS = 4
-DETOUR = 256
+DETOUR_LOW, DETOUR_HIGH = 384, 256
 
 
 def gelu_tanh(c):
@@ -46,8 +46,8 @@
     last = chunks - 1
     low, high = cy == 0, cy == 1
     kept = half - SKEW
-    source, sink = (cz == 0) & (cx == 0) & high, (cz == 0) & (cx == 0) & low
-    relay_high, relay_low = (cz == 1) & (cx == 0) & high, (cz == 1) & (cx == 0) & low
+    source, relay = (cz == 0) & (cx == 0), (cz == 1) & (cx == 0)
+    sides = ((high, DETOUR_LOW, DETOUR_HIGH), (low, DETOUR_HIGH, DETOUR_LOW))
 
     x_first = pltpu.make_async_copy(x.at[pl.ds(0, M)], xv.at[pl.ds(0, M)], xl_sem.at[0])
     x_last = pltpu.make_async_copy(x.at[pl.ds(M, rows - M)], xv.at[pl.ds(10 * M, rows - M)], xl_sem.at[0])
@@ -105,10 +105,8 @@
         c = pl.ds(*FIRST[k])
         return remote(ps.at[pl.ds(0, M), c], pr.at[pl.ds(0, M), c], p_send.at[0], p_recv.at[0], across)
 
-    straight = half - DETOUR
-
-    def p_straight():
-        c = pl.ds(0, straight)
+    def p_straight(width):
+        c = pl.ds(0, half - width)
         return remote(ps.at[at(last - 1), c], pr.at[at(last - 1), c], p_send.at[1], p_recv.at[(last - 1) % SLOTS], across)
 
     def p_whole():
@@ -124,11 +122,13 @@
         c = pl.ds(0, kept)
         return remote(ps.at[at(last), c], pr.at[at(last), c], p_send.at[2], p_recv.at[last % SLOTS], across)
 
-    detour = [
-        remote(ra, rb, r_send.at[0], r_recv.at[0], along),
-        remote(rb, rc, r_send.at[0], r_recv.at[0], across),
-        remote(rc, pr.at[at(last - 1), pl.ds(straight, DETOUR)], r_send.at[0], r_recv.at[0], along),
-    ]
+    def detour(hop, width):
+        c, end = pl.ds(0, width), pl.ds(half - width, width)
+        if hop == 0:
+            return remote(ra.at[:, c], rb.at[:, c], r_send.at[0], r_recv.at[0], along)
+        if hop == 1:
+            return remote(rb.at[:, c], rc.at[:, c], r_send.at[0], r_recv.at[1], across)
+        return remote(rc.at[:, c], pr.at[at(last - 1), end], r_send.at[0], r_recv.at[0], along)
 
     def h_piece(k, piece):
         c = pl.ds(*piece)
@@ -144,12 +144,11 @@
 
     x_first.start()
     w1_send[0].start()
+    w1_send[1].start()
     x_first.wait()
     for k in range(parts):
         c = pl.ds(*FIRST[k])
         w1_send[k].wait()
-        if k == 0:
-            w1_send[1].start()
         if k < parts - 2:
             w1_send[k + 2].start()
         ps[pl.ds(0, M), c] = jnp.dot(xv[pl.ds(0, M), :], w1v[0, :, c], preferred_element_type=F32)
@@ -201,9 +200,10 @@
         def _():
             p_copy(i).start()
 
-        @pl.when(source & (i == last - 1))
-        def _():
-            p_straight().start()
+        for side, width, _ in sides:
+            @pl.when(source & side & (i == last - 1))
+            def _():
+                p_straight(width).start()
 
         @pl.when(~source & (i == last - 1))
         def _():
@@ -224,14 +224,15 @@
     def hidden(i):
         first_layer(i, 1, po, pl.ds(0, M))
 
-        @pl.when(~sink | (i < last - 1))
+        @pl.when(~source | (i < last - 1))
         def _():
             p_copy(i).wait_recv()
 
-        @pl.when(sink & (i == last - 1))
-        def _():
-            p_straight().wait_recv()
-            detour[2].wait_recv()
+        for side, _, width in sides:
+            @pl.when(source & side & (i == last - 1))
+            def _():
+                p_straight(width).wait_recv()
+                detour(2, width).wait_recv()
 
         for n in range(tiles):
             activate(i, pl.ds(n * TILE, TILE))
@@ -311,20 +312,23 @@
             multiply(hr, kept, SKEW, half, add)
 
     def step(t, carry):
-        @pl.when(source & (t == 3))
-        def _():
-            ra[...] = jnp.dot(xv[at(last - 1), :], w1v[0, :, pl.ds(straight, DETOUR)], preferred_element_type=F32)
-            detour[0].start()
-
-        @pl.when(relay_high & (t == 4))
-        def _():
-            detour[0].wait_recv()
-            detour[1].start()
-
-        @pl.when(relay_low & (t == 7))
-        def _():
-            detour[1].wait_recv()
-            detour[2].start()
+        for side, width, back in sides:
+            @pl.when(source & side & (t == 3))
+            def _():
+                end = pl.ds(half - width, width)
+                ra[:, pl.ds(0, width)] = jnp.dot(xv[at(last - 1), :], w1v[0, :, end], preferred_element_type=F32)
+                detour(0, width).start()
+
+            @pl.when(relay & side & (t == 4))
+            def _():
+                detour(0, width).wait_recv()
+                detour(1, width).start()
+
+            @pl.when(relay & side & (t == 7))
+            def _():
+                detour(1, back).wait_recv()
+                detour(1, width).wait_send()
+                detour(2, back).start()
 
         @pl.when(t < chunks)
         def _():
@@ -401,10 +405,15 @@
     most = pl.ds(0, last * M)
     remote(ho.at[most], hr.at[most], h_send.at[0], h_recv.at[0], across).wait_send()
 
-    @pl.when(source)
-    def _():
-        p_straight().wait_send()
-        detour[0].wait_send()
+    for side, width, back in sides:
+        @pl.when(source & side)
+        def _():
+            p_straight(width).wait_send()
+            detour(0, width).wait_send()
+
+        @pl.when(relay & side)
+        def _():
+            detour(2, back).wait_send()
 
     @pl.when(~source)
     def _():
@@ -421,14 +430,6 @@
         p_low().wait_send()
         h_over().wait_send()
         h_piece(0, (0, half)).wait_send()
-
-    @pl.when(relay_high)
-    def _():
-        detour[1].wait_send()
-
-    @pl.when(relay_low)
-    def _():
-        detour[2].wait_send()
 
 
 def solution(mesh):
@@ -452,16 +453,16 @@
                 pltpu.VMEM((total, half), BF16),
                 pltpu.VMEM((total, half), F32),
                 pltpu.VMEM((3 * rows, half), F32),
-                pltpu.VMEM((M, DETOUR), F32),
-                pltpu.VMEM((M, DETOUR), F32),
-                pltpu.VMEM((M, DETOUR), F32),
+                pltpu.VMEM((M, max(DETOUR_LOW, DETOUR_HIGH)), F32),
+                pltpu.VMEM((M, max(DETOUR_LOW, DETOUR_HIGH)), F32),
+                pltpu.VMEM((M, max(DETOUR_LOW, DETOUR_HIGH)), F32),
                 pltpu.VMEM((M, SKEW), F32),
                 pltpu.VMEM((M, SKEW), F32),
                 dma(1), dma(2), dma(1),
                 dma(1), dma(1), dma(1), dma(1),
                 dma(1), dma(2), dma(1), dma(1),
                 dma(4), dma(SLOTS + 1), dma(3), dma(SLOTS + len(TO_LOW) + 1),
-                dma(1), dma(1), dma(1), dma(1),
+                dma(1), dma(1), dma(1), dma(2),
             ],
             compiler_params=pltpu.CompilerParams(
                 collective_id=0, has_side_effects=True, vmem_limit_bytes=48 * 1024 * 1024

time: 158 us -> 157 us (level)
  no operation moved by 1% of the time
where the time goes in v8:
time: 157 us
  Pallas kernels  156 us (99%)
    pallas_call x1, Pallas kernels, body(): pl.pallas_call(kernel, out_shape=jax.ShapeDtypeStruct((rows, half), BF16)...  156 us

profile of v8, /device:TPU:0, one launch (start us, length us, event | category | flops | bytes accessed | tf_op | source)
XLA Modules:
  0.0 156.7 jit_solution(8816736932429503292)
XLA Ops:
  0.0 155.9 %shard_map.37 = bf16[192,1536]{1,0:T(8,128)(2,1)S(1)} custom-call(bf16[192,1536]{1,0:T(8,128)(2,1)} %x.1, bf16[1536,3072]{1,0:T(8,128)(2,1)} %w1.1, bf16[6144,768]{1,0:T(8,128)(2,1)} %w2.1), custom_call_target="tpu_custom_call" | custom-call | tf_op jit(solution)/shard_map/pallas_call | solution.py:440
  155.9 0.8 copy.5

commit v9 on v8

--- a/solution.py
+++ b/solution.py
@@ -25,8 +25,8 @@
 
 
 def kernel(x, w1, w2, z, xv, w1v, w2v, ps, pr, po, ho, hr, zs, zr, ra, rb, rc, pe, pq,
-           xl_sem, w1_sem, w2_sem, bx_send, bx_recv, bw_send, bw_recv,
-           xy_send, xy_recv, xf_send, xf_recv, p_send, p_recv, h_send, h_recv, z_send, z_recv, r_send, r_recv):
+           w1_sem, bx_recv, bw_recv,
+           xy_send, xy_recv, xf_recv, p_send, p_recv, h_send, h_recv, z_send, z_recv, r_send, r_recv):
     cz, cy, cx = lax.axis_index("cz"), lax.axis_index("cy"), lax.axis_index("cx")
     across = {"cy": 1 - cy}
     partner = {"cx": 1 - cx}
@@ -49,8 +49,8 @@
     source, relay = (cz == 0) & (cx == 0), (cz == 1) & (cx == 0)
     sides = ((high, DETOUR_LOW, DETOUR_HIGH), (low, DETOUR_HIGH, DETOUR_LOW))
 
-    x_first = pltpu.make_async_copy(x.at[pl.ds(0, M)], xv.at[pl.ds(0, M)], xl_sem.at[0])
-    x_last = pltpu.make_async_copy(x.at[pl.ds(M, rows - M)], xv.at[pl.ds(10 * M, rows - M)], xl_sem.at[0])
+    x_first = pltpu.make_async_copy(x.at[pl.ds(0, M)], xv.at[pl.ds(0, M)], w1_sem.at[2])
+    x_last = pltpu.make_async_copy(x.at[pl.ds(M, rows - M)], xv.at[pl.ds(10 * M, rows - M)], w1_sem.at[1])
     tiles = half // TILE
 
     def w1_cols(side, start, width):
@@ -68,26 +68,25 @@
     mine = pl.ds(pl.multiple_of(cx * width, width), width)
     both = pl.ds(0, 2 * half)
     w2_half = [pl.ds(k * half, half) for k in range(2)]
-    w2_local = [pltpu.make_async_copy(w2_rows(cx, k), w2v.at[w2_half[k], mine], w2_sem.at[0]) for k in range(2)]
-    w2_local_all = pltpu.make_async_copy(w2.at[both], w2v.at[:, mine], w2_sem.at[0])
-    w2_swap = [remote(w2_rows(1 - cx, k), w2v.at[w2_half[k], mine], bw_send.at[0], bw_recv.at[0], partner)
+    w2_local = [pltpu.make_async_copy(w2_rows(cx, k), w2v.at[w2_half[k], mine], w1_sem.at[2]) for k in range(2)]
+    w2_local_all = pltpu.make_async_copy(w2.at[both], w2v.at[:, mine], w1_sem.at[2])
+    w2_swap = [remote(w2_rows(1 - cx, k), w2v.at[w2_half[k], mine], xy_send.at[0], bw_recv.at[0], partner)
                for k in range(2)]
-    w2_swap_all = remote(w2.at[both], w2v.at[:, mine], bw_send.at[0], bw_recv.at[0], partner)
+    w2_swap_all = remote(w2.at[both], w2v.at[:, mine], xy_send.at[0], bw_recv.at[0], partner)
     x_swap = [
-        remote(x.at[pl.ds(0, M)], xv.at[pl.ds(M, M)], bx_send.at[0], bx_recv.at[0], partner),
-        remote(x.at[pl.ds(M, rows - M)], xv.at[pl.ds(8 * M, rows - M)], bx_send.at[0], bx_recv.at[0], partner),
+        remote(x.at[pl.ds(0, M)], xv.at[pl.ds(M, M)], xy_send.at[0], bx_recv.at[0], partner),
+        remote(x.at[pl.ds(M, rows - M)], xv.at[pl.ds(8 * M, rows - M)], xy_send.at[0], bx_recv.at[0], partner),
     ]
-    x_swap_all = remote(x, xv.at[pl.ds(7 * M, rows)], bx_send.at[0], bx_recv.at[0], partner)
+    x_swap_all = remote(x, xv.at[pl.ds(7 * M, rows)], xy_send.at[0], bx_recv.at[0], partner)
     x_along = [
         remote(x.at[pl.ds(0, M)], xv.at[pl.ds(2 * M, M)], xy_send.at[0], xy_recv.at[0], along),
         remote(x.at[pl.ds(M, rows - M)], xv.at[pl.ds(3 * M, rows - M)], xy_send.at[0], xy_recv.at[1], along),
     ]
-    x_along_all = remote(x, xv.at[pl.ds(2 * M, rows)], xy_send.at[0], xy_recv.at[0], along)
     x_forward = [
-        remote(xv.at[pl.ds(2 * M, M)], xv.at[pl.ds(5 * M, M)], xf_send.at[0], xf_recv.at[0], partner),
-        remote(xv.at[pl.ds(3 * M, rows - M)], xv.at[pl.ds(6 * M, rows - M)], xf_send.at[0], xf_recv.at[0], partner),
+        remote(xv.at[pl.ds(2 * M, M)], xv.at[pl.ds(5 * M, M)], xy_send.at[0], xf_recv.at[0], partner),
+        remote(xv.at[pl.ds(3 * M, rows - M)], xv.at[pl.ds(6 * M, rows - M)], xy_send.at[0], xf_recv.at[0], partner),
     ]
-    x_forward_all = remote(xv.at[pl.ds(2 * M, rows)], xv.at[pl.ds(5 * M, rows)], xf_send.at[0], xf_recv.at[0], partner)
+    x_forward_all = remote(xv.at[pl.ds(2 * M, rows)], xv.at[pl.ds(5 * M, rows)], xy_send.at[0], xf_recv.at[0], partner)
 
     def p_copy(i):
         return remote(ps.at[at(i)], pr.at[at(i)], p_send.at[0], p_recv.at[i % SLOTS], across)
@@ -116,7 +115,7 @@
         return remote(ps.at[at(last)], pr.at[at(last)], p_send.at[2], p_recv.at[last % SLOTS], across)
 
     def p_over():
-        return remote(pe, pq, p_send.at[3], p_recv.at[SLOTS], across)
+        return remote(pe, pq, h_send.at[2], h_recv.at[SLOTS + len(TO_LOW)], across)
 
     def p_low():
         c = pl.ds(0, kept)
@@ -398,8 +397,9 @@
     def _():
         close_pieces(TO_HIGH)
 
-    for copy in (x_along_all, x_swap_all, w2_swap_all, x_forward_all, z_all):
-        copy.wait_send()
+    z_all.wait_send()
+    sent = pl.ds(0, 3 * rows + half)
+    remote(w2v.at[sent], w2v.at[pl.ds(half - 3 * rows, 3 * rows + half)], xy_send.at[0], xy_recv.at[0], along).wait_send()
     most = pl.ds(0, (last - 1) * M)
     remote(ps.at[most], pr.at[most], p_send.at[0], p_recv.at[0], across).wait_send()
     most = pl.ds(0, last * M)
@@ -458,10 +458,10 @@
                 pltpu.VMEM((M, max(DETOUR_LOW, DETOUR_HIGH)), F32),
                 pltpu.VMEM((M, SKEW), F32),
                 pltpu.VMEM((M, SKEW), F32),
+                dma(3),
+                dma(1), dma(1),
                 dma(1), dma(2), dma(1),
-                dma(1), dma(1), dma(1), dma(1),
-                dma(1), dma(2), dma(1), dma(1),
-                dma(4), dma(SLOTS + 1), dma(3), dma(SLOTS + len(TO_LOW) + 1),
+                dma(3), dma(SLOTS), dma(3), dma(SLOTS + len(TO_LOW) + 1),
                 dma(1), dma(1), dma(1), dma(2),
             ],
             compiler_params=pltpu.CompilerParams(

time: 157 us -> 157 us (level)
  no operation moved by 1% of the time
where the time goes in v9:
time: 157 us
  Pallas kernels  156 us (99%)
    pallas_call x1, Pallas kernels, body(): pl.pallas_call(kernel, out_shape=jax.ShapeDtypeStruct((rows, half), BF16)...  156 us

profile of v9, /device:TPU:0, one launch (start us, length us, event | category | flops | bytes accessed | tf_op | source)
XLA Modules:
  0.0 156.7 jit_solution(13379378861370895414)
XLA Ops:
  0.0 155.8 %shard_map.37 = bf16[192,1536]{1,0:T(8,128)(2,1)S(1)} custom-call(bf16[192,1536]{1,0:T(8,128)(2,1)} %x.1, bf16[1536,3072]{1,0:T(8,128)(2,1)} %w1.1, bf16[6144,768]{1,0:T(8,128)(2,1)} %w2.1), custom_call_target="tpu_custom_call" | custom-call | tf_op jit(solution)/shard_map/pallas_call | solution.py:440
  155.8 0.8 copy.5

commit v10 on v9

--- a/solution.py
+++ b/solution.py
@@ -17,7 +17,7 @@
 TO_LOW = ((0, 768), (768, 512), (1280, 256))
 TO_HIGH = ((0, 768), (768, 256), (1024, 256))
 SLOTS = 4
-DETOUR_LOW, DETOUR_HIGH = 384, 256
+DETOUR_LOW, DETOUR_HIGH = 384, 128
 
 
 def gelu_tanh(c):

time: 157 us -> 157 us (level)
  no operation moved by 1% of the time
where the time goes in v10:
time: 157 us
  Pallas kernels  156 us (99%)
    pallas_call x1, Pallas kernels, body(): pl.pallas_call(kernel, out_shape=jax.ShapeDtypeStruct((rows, half), BF16)...  156 us

profile of v10, /device:TPU:0, one launch (start us, length us, event | category | flops | bytes accessed | tf_op | source)
XLA Modules:
  0.0 157.0 jit_solution(1341423311213643683)
XLA Ops:
  0.0 156.2 %shard_map.37 = bf16[192,1536]{1,0:T(8,128)(2,1)S(1)} custom-call(bf16[192,1536]{1,0:T(8,128)(2,1)} %x.1, bf16[1536,3072]{1,0:T(8,128)(2,1)} %w1.1, bf16[6144,768]{1,0:T(8,128)(2,1)} %w2.1), custom_call_target="tpu_custom_call" | custom-call | tf_op jit(solution)/shard_map/pallas_call | solution.py:440
  156.2 0.8 copy.5
